TPU v7x, 32 devices: a whole 2x2x4 slice. The times are simulated.
32 devices in a mesh: band: 2 (over x), domain: 16 (over z, y, core).
Axes of the slice: x: 2, y: 2, z: 4, core: 2. Of those that a mesh axis runs over, the one named last changes fastest.
Arguments:
- dens_part: float32 [2, 171, 36864], P('band', None, 'domain'), may hold values from -3 to 3
- counts: int32 [16], P('domain'), may hold values from 1 to 2304, 12288 in all
- gaunt: float32 [171, 525], replicated, may hold values from -0.4375 to 0.4375
- pair_waves: float32 [21, 400], replicated, may hold values from -1.25 to 1.25
- y_table: float32 [25, 50], replicated, may hold values from -1.25 to 1.25
- core: float32 [400], replicated, may hold values from 1 to 4
- radial_weights: float32 [400], replicated, may hold values from 0.0001 to 0.001
Outputs:
- dh_packed: float32 [171, 36864], P(None, 'domain')
- atom_energy: float32 [36864], P('domain')
Inputs may be any that keep to these rules, and one draw needn't show every extreme that they name: `counts`: atoms owned by each domain; they sum to 12288, and some domain owns exactly 2304.
All inputs are finite; a program needn't handle non-finite values. No bound on the sum of `counts` on one device may be relied on, other than what follows from the above.
Results may differ from a plain program's by a relative error of at most 0.0003.
Values sent between devices are 32-bit elements; how exact they have to be, the bound alone decides.
A program may use at most 128 MiB of HBM per device.

v0:
```python
import math

import jax
import jax.numpy as jnp
from jax import lax
from jax.experimental import pallas as pl
from jax.experimental.pallas import tpu as pltpu
from jax.sharding import PartitionSpec as P

highest = lax.Precision.HIGHEST
f32 = jnp.float32
bf16 = jnp.bfloat16

LANES = 128
WIDE = 256

C_RS = 0.6203504908994
EX_A = 0.7385587663820224
EX_D = 0.9847450218426965

def round_up(value, step):
    return -(-value // step) * step

def split(x):
    hi = lax.reduce_precision(x, 8, 7)
    return hi.astype(bf16), (x - hi).astype(bf16)

def atom_kernel(
    dens_ref, gy_ref, gyb_ref, pw_ref, pwb_ref, core_ref, weight_ref,
    ham_ref, energy_ref, pts_ref, hi_ref, lo_ref, eacc_ref, back_ref, *, pairs, step
):
    atoms = dens_ref.shape[1]
    rows = pw_ref.shape[1]
    grid_points = pw_ref.shape[0]
    couples = gy_ref.shape[0]
    chunks = 2 * atoms // WIDE
    eacc_ref[...] = jnp.zeros_like(eacc_ref)

    def mixed(x):
        ids = lax.broadcasted_iota(jnp.int32, x.shape, 0)
        hi = x.astype(bf16).astype(f32)
        low = (ids >= pairs) & (ids < 2 * pairs)
        return jnp.where(low, x - hi, hi).astype(bf16)

    def body(m, carry):
        both = jnp.dot(gy_ref[m], dens_ref[...], preferred_element_type=f32)
        lhs = mixed(jnp.concatenate([both[:rows], both[rows:]], axis=1))
        back = []
        for j in range(chunks):
            cols = lhs[:, j * WIDE:(j + 1) * WIDE]
            pts_ref[j] = jnp.dot(pw_ref[...], cols, preferred_element_type=f32)
            for g in range(0, grid_points, step):
                part = pl.ds(g, step)
                p = pts_ref[j, part, :] + core_ref[part, :]
                u = p * p + 0.25
                v = jnp.exp2(jnp.log(u) * (-1.0 / (6.0 * math.log(2.0))))
                r = v / (7.8 + C_RS * v)
                v2 = v * v
                br = 0.44 * r
                eacc_ref[j, part, :] += (u * v2) * (EX_A + br)
                pot = (p * v2) * (EX_D + (0.44 + (0.44 * C_RS / 3.0) * r) * r)
                hi = pot.astype(bf16)
                hi_ref[j, part, :] = hi
                lo_ref[j, part, :] = (pot - hi.astype(f32)).astype(bf16)
            first = jnp.dot(pwb_ref[...], hi_ref[j], preferred_element_type=f32)
            second = jnp.dot(pwb_ref[:rows, :], lo_ref[j], preferred_element_type=f32)
            back.append(first[:rows] + first[rows:] + second)
        back = mixed(jnp.concatenate(back, axis=1))
        start = pl.multiple_of(m * 2 * rows, 2 * rows)
        back_ref[pl.ds(start, rows), :] = back[:, :atoms]
        back_ref[pl.ds(start + rows, rows), :] = back[:, atoms:]
        return carry

    lax.fori_loop(0, couples, body, 0)
    ham_ref[...] = jnp.dot(gyb_ref[...], back_ref[...], preferred_element_type=f32)
    sums = [
        jnp.sum(eacc_ref[j] * weight_ref[...], axis=0, keepdims=True) for j in range(chunks)
    ]
    sums = jnp.concatenate(sums, axis=1)
    energy_ref[...] = jnp.broadcast_to(
        -(sums[:, :atoms] + sums[:, atoms:]), energy_ref.shape
    )

def prepare(gaunt, pair_waves, y_table, core, radial_weights):
    entries = gaunt.shape[0]
    harmonics, directions = y_table.shape
    pairs, grid_points = pair_waves.shape
    rows = round_up(3 * pairs, 16)
    extra = rows - 3 * pairs
    assert directions % 2 == 0
    fused = jnp.einsum(
        "plq,ln->nqp", gaunt.reshape(entries, harmonics, pairs), y_table, precision=highest
    )

    hi, lo = split(fused)
    wide = lambda a, b, c: jnp.pad(
        jnp.concatenate([a, b, c], axis=1), ((0, 0), (0, extra), (0, 0))
    )
    hi3 = wide(hi, hi, hi)
    lo3 = wide(lo, lo, lo)
    gy = jnp.concatenate([hi3, hi3, lo3], axis=2).reshape(directions // 2, 2 * rows, 3 * entries)
    gyb = wide(hi, hi, lo).reshape(directions * rows, entries).T
    pw_hi, pw_lo = split(pair_waves)
    pw = jnp.pad(jnp.concatenate([pw_hi, pw_hi, pw_lo], axis=0), ((0, extra), (0, 0))).T
    point_weight = 4.0 * jnp.pi / directions * radial_weights
    b_hi, b_lo = split(-point_weight[None, :] * pair_waves)
    triple = lambda x: jnp.pad(jnp.concatenate([x, x, x], axis=0), ((0, extra), (0, 0)))
    pwb = jnp.concatenate([triple(b_hi), triple(b_lo)], axis=0)
    core_wide = jnp.broadcast_to(core[:, None], (grid_points, WIDE))
    weight_wide = jnp.broadcast_to(point_weight[:, None], (grid_points, WIDE))
    return gy, gyb, pw, pwb, core_wide, weight_wide

def local_energy(columns, tables, pairs):
    entries, atoms = columns.shape
    gy, gyb, pw, pwb, core_wide, weight_wide = tables
    grid_points, rows = pw.shape
    hi, lo = split(columns)
    dens = jnp.concatenate([hi, lo, hi], axis=0)
    chunks = 2 * atoms // WIDE
    step = 80 if grid_points % 80 == 0 else grid_points

    ham, energy = pl.pallas_call(
        lambda *refs: atom_kernel(*refs, pairs=pairs, step=step),
        out_shape=(
            jax.ShapeDtypeStruct((entries, atoms), f32),
            jax.ShapeDtypeStruct((8, atoms), f32),
        ),
        scratch_shapes=[
            pltpu.VMEM((chunks, grid_points, WIDE), f32),
            pltpu.VMEM((chunks, grid_points, WIDE), bf16),
            pltpu.VMEM((chunks, grid_points, WIDE), bf16),
            pltpu.VMEM((chunks, grid_points, WIDE), f32),
            pltpu.VMEM((gyb.shape[1], atoms), bf16),
        ],
        compiler_params=pltpu.CompilerParams(vmem_limit_bytes=48 * 1024 * 1024),
        name="atoms",
    )(dens, gy, gyb, pw, pwb, core_wide, weight_wide)
    return ham, energy[:1]

def per_device(dens_part, counts, gaunt, pair_waves, y_table, core, radial_weights):
    band_count = lax.axis_size("band")
    domain_count = lax.axis_size("domain")
    workers = band_count * domain_count
    axes = ("domain", "band")
    me = lax.axis_index("domain") * band_count + lax.axis_index("band")
    entries = dens_part.shape[1]
    slot_total = dens_part.shape[2]
    share = slot_total // band_count
    capacity = -(-share // workers)
    worker_rows = -(-(slot_total // 3) // band_count)
    atoms = round_up(worker_rows, LANES)
    tables = prepare(gaunt, pair_waves, y_table, core, radial_weights)

    own_cols = lax.psum_scatter(dens_part[0], "band", scatter_dimension=1, tiled=True)
    every_count = lax.all_gather(counts, "domain", axis=0, tiled=True)
    band_ids = jnp.arange(band_count, dtype=jnp.int32)
    live = jnp.clip(every_count[:, None] - band_ids[None, :] * share, 0, share).reshape(-1)
    ids = jnp.arange(workers, dtype=jnp.int32)
    starts = jnp.sum(jnp.where(ids[None, :] < ids[:, None], live[None, :], 0), axis=1)
    ends = starts + live
    own_start = jnp.sum(jnp.where(ids == me, starts, 0))
    own_live = jnp.sum(jnp.where(ids == me, live, 0))
    is_alive = jnp.arange(share, dtype=jnp.int32) < own_live

    own_cols = jnp.where(is_alive[None, :], own_cols, 0.0)
    own_cols = jnp.pad(own_cols, ((0, 0), (0, capacity * workers - share)))
    blocks = own_cols.T.reshape(capacity, workers, entries).transpose(1, 0, 2)
    outgoing = jnp.roll(blocks, own_start % workers, axis=0)
    incoming = lax.all_to_all(outgoing, axes, split_axis=0, concat_axis=0, tiled=True)

    atom_ids = jnp.arange(atoms, dtype=jnp.int32) * workers + me
    source = jnp.sum((ends[None, :] <= atom_ids[:, None]).astype(jnp.int32), axis=1)
    source = jnp.minimum(source, workers - 1)
    source_start = jnp.sum(jnp.where(source[:, None] == ids[None, :], starts[None, :], 0), axis=1)
    position = jnp.clip((atom_ids - source_start) // workers, 0, capacity - 1)
    compact = jnp.take(
        incoming.reshape(workers * capacity, entries), source * capacity + position, axis=0,
        mode="clip",
    )
    ham, energy = local_energy(compact.T, tables, pair_waves.shape[0])
    result = jnp.concatenate([ham, energy], axis=0).T
    row = (me - starts) % workers
    first = (starts + row - me) // workers
    target = first[:, None] + jnp.arange(capacity, dtype=jnp.int32)[None, :]
    back = jnp.take(result, jnp.clip(target, 0, atoms - 1).reshape(-1), axis=0, mode="clip")
    returned = lax.all_to_all(
        back.reshape(workers, capacity, entries + 1), axes, split_axis=0, concat_axis=0, tiled=True
    )
    returned = jnp.roll(returned, -(own_start % workers), axis=0)
    piece = returned.transpose(1, 0, 2).reshape(capacity * workers, entries + 1)[:share]
    piece = jnp.where(is_alive[:, None], piece, 0.0)
    band = lax.axis_index("band")
    whole = jnp.zeros((slot_total, entries + 1), f32)
    ring = [(i, (i + 1) % band_count) for i in range(band_count)]
    for hop in range(band_count):
        owner = (band - hop) % band_count
        whole = lax.dynamic_update_slice(whole, piece, (owner * share, 0))
        if hop + 1 < band_count:
            piece = lax.ppermute(piece, "band", ring)
    whole = whole.T
    return whole[:entries], whole[entries]

def solution(mesh):
    return jax.shard_map(
        per_device,
        mesh=mesh,
        in_specs=(P("band", None, "domain"), P("domain"), P(), P(), P(), P(), P()),
        out_specs=(P(None, "domain"), P("domain")),
        check_vma=False,
    )
```

profile of v0, /device:TPU:0, one launch (start us, length us, event | category | flops | bytes accessed | tf_op | source)
XLA Modules:
  0.0 206.9 jit_solution(14510031939647462586)
XLA Ops:
  7.2 5.1 %copy.60 = f32[1,171,2304]{1,2,0:T(8,128)} copy(f32[1,171,2304]{2,0,1:T(1,128)} %param.7) | data formatting | bytes 3151872 | tf_op args[0]
  13.6 0.8 dynamic-update-slice
  14.4 13.8 %all-reduce.6 = s32[16]{0:T(128)S(1)} all-reduce(s32[16]{0:T(128)S(1)} %dynamic-update-slice), channel_id=1, replica_groups=mesh['band'=2,'domain'=16] {'domain'}, use_global_device_ids=true, to_apply=%add.6 | all-reduce | flops 16 | bytes 128
  28.2 0.7 select_reduce_fusion.2
  32.0 1.2 reduce-precision_convert_fusion
  33.2 0.9 pad_maximum_fusion
  34.4 3.1 %fusion.1 = bf16[50,64,513]{2,0,1:T(8,128)(2,1)S(1)} fusion(bf16[50,63,171]{2,0,1:T(8,128)(2,1)S(1)} %get-tuple-element.10, bf16[50,64,171]{2,0,1:T(8,128)(2,1)S(1)} %pad.20), kind=kLoop, calls=%fused_computation.4 | loop fusion | flops 13132800 | bytes 5454900 | tf_op jit(solution)/shard_map/concatenate | solution.py:101
  37.6 2.7 %copy.65 = bf16[50,64,513]{2,1,0:T(8,128)(2,1)} copy(bf16[50,64,513]{2,0,1:T(8,128)(2,1)S(1)} %fusion.1) | data formatting | bytes 6566400 | tf_op jit(solution)/shard_map/concatenate | solution.py:101
  41.4 1.0 copy.67
  43.0 7.0 %reduce-scatter.2.cloned.1.call-done = f32[171,1152]{0,1:T(8,128)} async-done(((f32[171,2304]{0,1:T(8,128)}), f32[171,1152]{0,1:T(8,128)}) %reduce-scatter.2.cloned.1.call-update) | async-done | bytes 787984 | tf_op jit(solution)/shard_map/reduce_scatter | solution.py:154
  50.0 1.5 broadcast_select_fusion
  51.9 1.7 copy.61
  53.6 4.9 %all-to-all-start = ((f32[32,36,171]{2,1,0:T(8,128)}), f32[32,36,171]{2,1,0:T(8,128)}, u32[]{:S(2)}, u32[]{:S(2)}) async-start(f32[32,36,171]{2,1,0:T(8,128)} %copy.61), calls=%async_computation.1 | async-start | bytes 2621440 | tf_op jit(solution)/shard_map/all_to_all | solution.py:169
  59.2 30.9 %all-to-all-done = f32[32,36,171]{2,1,0:T(8,128)} async-done(((f32[32,36,171]{2,1,0:T(8,128)}), f32[32,36,171]{2,1,0:T(8,128)}, u32[]{:S(2)}, u32[]{:S(2)}) %all-to-all-start) | async-done | bytes 788000 | tf_op jit(solution)/shard_map/all_to_all | solution.py:169
  90.2 1.4 reshape.223
  91.6 1.7 gather_fusion
  94.1 43.6 %atoms.1 = (f32[171,384]{1,0:T(8,128)S(1)}, f32[8,384]{1,0:T(8,128)S(1)}) custom-call(bf16[513,384]{1,0:T(8,128)(2,1)S(1)} %pad_maximum_fusion.4.refs_0_, bf16[25,128,513]{2,1,0:T(8,128)(2,1)} %bitcast.33, bf16[171,3200]{1,0:T(8,128)(2,1)S(1)} %bitcast.32, bf16[400,64]{1,0:T(8,128)(2,1)S(1)} %fusion.19.refs_3_, ...), custom_call_target="tpu_custom_call" | custom-call | tf_op jit(solution)/shard_map/atoms/pallas_call | solution.py:122
  137.9 3.3 %gather_fusion.1 = f32[1152,172]{1,0:T(8,128)S(1)} fusion(f32[384,172]{1,0:T(8,128)S(1)} %copy.71, s32[2048]{0:T(1024)S(1)} %pad_clamp_fusion), kind=kCustom, calls=%fused_computation.1 | custom fusion | bytes 1589760 | tf_op jit(solution)/shard_map/jit(_take)/gather | solution.py:185
  141.2 1.2 reshape.227
  142.4 3.6 %all-to-all-start.1 = ((f32[32,36,172]{2,1,0:T(8,128)}), f32[32,36,172]{2,1,0:T(8,128)S(1)}, u32[]{:S(2)}, u32[]{:S(2)}) async-start(f32[32,36,172]{2,1,0:T(8,128)} %reshape.227), calls=%async_computation.2 | async-start | bytes 2621440 | tf_op jit(solution)/shard_map/all_to_all | solution.py:186
  146.0 31.8 %all-to-all-done.1 = f32[32,36,172]{2,1,0:T(8,128)S(1)} async-done(((f32[32,36,172]{2,1,0:T(8,128)}), f32[32,36,172]{2,1,0:T(8,128)S(1)}, u32[]{:S(2)}, u32[]{:S(2)}) %all-to-all-start.1) | async-done | bytes 792608 | tf_op jit(solution)/shard_map/all_to_all | solution.py:186
  179.2 1.6 collective-permute-start
  180.9 17.9 %collective-permute-done = f32[1152,172]{0,1:T(8,128)S(1)} collective-permute-done((f32[1152,172]{0,1:T(8,128)S(1)}, f32[1152,172]{0,1:T(8,128)S(1)}, u32[]{:S(2)}, u32[]{:S(2)}) %collective-permute-start) | collective-permute-done | bytes 792608 | tf_op jit(solution)/shard_map/ppermute | solution.py:199
  198.9 0.7 slice_reduce_fusion
  (61 shorter events, 7.8 us)
Async XLA Ops:
  7.2 24.8 %copy-start = (f32[25,50]{1,0:T(8,128)S(1)}, f32[25,50]{1,0:T(8,128)}, u32[]{:S(2)}) copy-start(f32[25,50]{1,0:T(8,128)} %param.11) | copy-start | bytes 15004
  7.2 42.8 %reduce-scatter.2.cloned.1.call-start = ((), (), s32[]{:S(2)}) async-start(), calls=%async_computation.3 | async-start | bytes 3538944 | tf_op jit(solution)/shard_map/reduce_scatter | solution.py:154
  12.3 0.7 copy-start.6
  12.3 19.4 %copy-start.2 = (f32[171,525]{1,0:T(8,128)S(1)}, f32[171,525]{1,0:T(8,128)}, u32[]{:S(2)}) copy-start(f32[171,525]{1,0:T(8,128)} %param.9) | copy-start | bytes 1077304
  37.5 2.7 %copy-start.3 = (f32[21,400]{1,0:T(8,128)S(1)}, f32[21,400]{1,0:T(8,128)}, u32[]{:S(2)}) copy-start(f32[21,400]{1,0:T(8,128)} %param.10) | copy-start | bytes 100804
  37.6 2.8 %copy-start.5 = (f32[400]{0:T(512)S(1)}, f32[400]{0:T(512)}, u32[]{:S(2)}) copy-start(f32[400]{0:T(512)} %param.13) | copy-start | bytes 4804
  53.6 36.5 %all-to-all-start = ((f32[32,36,171]{2,1,0:T(8,128)}), f32[32,36,171]{2,1,0:T(8,128)}, u32[]{:S(2)}, u32[]{:S(2)}) async-start(f32[32,36,171]{2,1,0:T(8,128)} %copy.61), calls=%async_computation.1 | async-start | bytes 2621440 | tf_op jit(solution)/shard_map/all_to_all | solution.py:169
  93.3 0.7 copy-start.4
  142.4 35.4 %all-to-all-start.1 = ((f32[32,36,172]{2,1,0:T(8,128)}), f32[32,36,172]{2,1,0:T(8,128)S(1)}, u32[]{:S(2)}, u32[]{:S(2)}) async-start(f32[32,36,172]{2,1,0:T(8,128)} %reshape.227), calls=%async_computation.2 | async-start | bytes 2621440 | tf_op jit(solution)/shard_map/all_to_all | solution.py:186
  179.2 19.6 %collective-permute-start = (f32[1152,172]{0,1:T(8,128)S(1)}, f32[1152,172]{0,1:T(8,128)S(1)}, u32[]{:S(2)}, u32[]{:S(2)}) collective-permute-start(f32[1152,172]{0,1:T(8,128)S(1)} %copy.73), channel_id=1, source_target_pairs={{0,16},{16,0},{1,17},{17,1},{2,18},{18,2},{3,19},{19,3},{4,20},{20... | collective-permute-start | bytes 2377736 | tf_op jit(solution)/shard_map/ppermute | solution.py:199
  198.9 1.2 copy-start.1
Sparse Core Ops, SparseCore 0:
  12.5 37.5 reduce-scatter.1
where the time goes:
time: 207 us
  waiting for transfers between devices  87.6 us (42%)
  Pallas kernels  43.6 us (21%)
  local copies, waits for them, and re-layouts  24.1 us (12%)
  between operations  17.1 us (8%)
  blocking collectives  13.8 us (7%)
  starting transfers between devices  10.1 us (5%)
  other arithmetic  9.25 us (4%)
    pallas_call x1, Pallas kernels, local_energy(): pl.pallas_call(lambda *refs: atom_kernel(*refs, pairs=pairs, step=step),...  43.6 us
    all_to_all x1, waiting for transfers between devices, per_device(): lax.all_to_all(back.reshape(workers, capacity, entries + 1), axes, split_...  31.8 us
    all_to_all x1, waiting for transfers between devices, per_device(): lax.all_to_all(outgoing, axes, split_axis=0, concat_axis=0, tiled=True)  30.9 us
    ppermute x1, waiting for transfers between devices, per_device(): piece = lax.ppermute(piece, 'band', ring)  17.9 us
    unnamed x1, blocking collectives  13.8 us
    unnamed x21, local copies, waits for them, and re-layouts  7.9 us
    reduce_scatter x1, waiting for transfers between devices, per_device(): lax.psum_scatter(dens_part[0], 'band', scatter_dimension=1, tiled=True)  6.99 us
    all_to_all x1, starting transfers between devices, per_device(): lax.all_to_all(outgoing, axes, split_axis=0, concat_axis=0, tiled=True)  4.9 us
  transfers between devices with their start and end apart: 4, of which 4 were waited for; matrix products, arithmetic and copies ran while one was open for 7% of the time, Pallas kernels for 0%

commit v1 on v0

--- a/solution.py
+++ b/solution.py
@@ -25,7 +25,7 @@
     hi = lax.reduce_precision(x, 8, 7)
     return hi.astype(bf16), (x - hi).astype(bf16)
 
-def atom_kernel(
+def general_kernel(
     dens_ref, gy_ref, gyb_ref, pw_ref, pwb_ref, core_ref, weight_ref,
     ham_ref, energy_ref, pts_ref, hi_ref, lo_ref, eacc_ref, back_ref, *, pairs, step
 ):
@@ -81,7 +81,7 @@
         -(sums[:, :atoms] + sums[:, atoms:]), energy_ref.shape
     )
 
-def prepare(gaunt, pair_waves, y_table, core, radial_weights):
+def general_tables(gaunt, pair_waves, y_table, core, radial_weights):
     entries = gaunt.shape[0]
     harmonics, directions = y_table.shape
     pairs, grid_points = pair_waves.shape
@@ -110,7 +110,7 @@
     weight_wide = jnp.broadcast_to(point_weight[:, None], (grid_points, WIDE))
     return gy, gyb, pw, pwb, core_wide, weight_wide
 
-def local_energy(columns, tables, pairs):
+def general_energy(columns, tables, pairs):
     entries, atoms = columns.shape
     gy, gyb, pw, pwb, core_wide, weight_wide = tables
     grid_points, rows = pw.shape
@@ -120,7 +120,7 @@
     step = 80 if grid_points % 80 == 0 else grid_points
 
     ham, energy = pl.pallas_call(
-        lambda *refs: atom_kernel(*refs, pairs=pairs, step=step),
+        lambda *refs: general_kernel(*refs, pairs=pairs, step=step),
         out_shape=(
             jax.ShapeDtypeStruct((entries, atoms), f32),
             jax.ShapeDtypeStruct((8, atoms), f32),
@@ -137,7 +137,7 @@
     )(dens, gy, gyb, pw, pwb, core_wide, weight_wide)
     return ham, energy[:1]
 
-def per_device(dens_part, counts, gaunt, pair_waves, y_table, core, radial_weights):
+def general(dens_part, counts, gaunt, pair_waves, y_table, core, radial_weights):
     band_count = lax.axis_size("band")
     domain_count = lax.axis_size("domain")
     workers = band_count * domain_count
@@ -149,7 +149,7 @@
     capacity = -(-share // workers)
     worker_rows = -(-(slot_total // 3) // band_count)
     atoms = round_up(worker_rows, LANES)
-    tables = prepare(gaunt, pair_waves, y_table, core, radial_weights)
+    tables = general_tables(gaunt, pair_waves, y_table, core, radial_weights)
 
     own_cols = lax.psum_scatter(dens_part[0], "band", scatter_dimension=1, tiled=True)
     every_count = lax.all_gather(counts, "domain", axis=0, tiled=True)
@@ -177,7 +177,7 @@
         incoming.reshape(workers * capacity, entries), source * capacity + position, axis=0,
         mode="clip",
     )
-    ham, energy = local_energy(compact.T, tables, pair_waves.shape[0])
+    ham, energy = general_energy(compact.T, tables, pair_waves.shape[0])
     result = jnp.concatenate([ham, energy], axis=0).T
     row = (me - starts) % workers
     first = (starts + row - me) // workers
@@ -200,7 +200,430 @@
     whole = whole.T
     return whole[:entries], whole[entries]
 
+MESH = pl.DeviceIdType.MESH
+SUBLANES = 8
+TAIL = 64
+
+def chunk_plan(slots, width):
+    windows = slots // width
+    return [range(k, min(k + 2, windows)) for k in range(0, windows, 2)]
+
+def dot_last(a, b):
+    return lax.dot_general(a, b, (((1,), (1,)), ((), ())), preferred_element_type=f32)
+
+def two(x):
+    hi = x.astype(bf16)
+    return hi, (x - hi.astype(f32)).astype(bf16)
+
+def greet(domains, domain, band):
+    barrier = pltpu.get_barrier_semaphore()
+
+    def hello(off, carry):
+        peer = lax.rem(domain + off, domains)
+        pl.semaphore_signal(barrier, inc=1, device_id=(band, peer), device_id_type=MESH)
+        return carry
+
+    lax.fori_loop(1, domains, hello, 0)
+    pl.semaphore_signal(barrier, inc=1, device_id=(1 - band, domain), device_id_type=MESH)
+    pl.semaphore_wait(barrier, domains)
+
+def scatter_kernel(
+    dens_ref, cnt_ref, recv_ref, all_ref, perm_ref, stage, send, cross,
+    cnt_out, cnt_in, x_out, x_in, a_out, a_in, *, domains
+):
+    band, domain = lax.axis_index("band"), lax.axis_index("domain")
+    entries, slots = dens_ref.shape
+    workers = 2 * domains
+    half = SUBLANES * domains
+    width = 2 * half
+    chunks = chunk_plan(slots, width)
+    extra = entries - LANES
+    greet(domains, domain, band)
+
+    def count_copy(off):
+        peer = lax.rem(domain + off, domains)
+        return pltpu.make_async_remote_copy(
+            src_ref=cnt_ref, dst_ref=all_ref.at[domain], send_sem=cnt_out.at[off],
+            recv_sem=cnt_in.at[off], device_id=(band, peer), device_id_type=MESH,
+        )
+
+    def loop(first, function):
+        def step(off, carry):
+            function(off)
+            return carry
+        lax.fori_loop(first, domains, step, 0)
+
+    loop(1, lambda off: count_copy(off).start())
+    all_ref[domain] = cnt_ref[...]
+    stage[...] = jnp.zeros_like(stage)
+    loop(1, lambda off: count_copy(off).wait_recv())
+    start = jnp.zeros((SUBLANES, LANES), jnp.int32)
+    for d in range(domains):
+        start = start + jnp.where(d < domain, all_ref[d], 0)
+    start = start[:1, :1]
+    row = lax.broadcasted_iota(jnp.int32, (width, width), 0)
+    slot = lax.broadcasted_iota(jnp.int32, (width, width), 1)
+    own = row < half
+    row = jnp.where(own, row, row - half)
+    worker = 2 * (row // SUBLANES) + jnp.where(own, band, 1 - band)
+    source = ((worker - start) & (workers - 1)) + workers * (row % SUBLANES)
+    perm = jnp.where(slot == source, 1.0, 0.0).astype(bf16)
+    perm_ref[...] = perm
+
+    def cross_copy(c):
+        lanes = (len(chunks[c]) + 1) * LANES
+        return pltpu.make_async_remote_copy(
+            src_ref=send.at[c, pl.ds(half, half), pl.ds(0, lanes)],
+            dst_ref=cross.at[c, :, pl.ds(0, lanes)], send_sem=x_out.at[c],
+            recv_sem=x_in.at[c], device_id=(1 - band, domain), device_id_type=MESH,
+        )
+
+    def deal_copy(c, off):
+        lanes = (len(chunks[c]) + 1) * LANES
+        peer = lax.rem(domain + off, domains)
+        rows = pl.ds(pl.multiple_of(peer * SUBLANES, SUBLANES), SUBLANES)
+        there = pl.ds(pl.multiple_of(domain * SUBLANES, SUBLANES), SUBLANES)
+        return pltpu.make_async_remote_copy(
+            src_ref=send.at[c, rows, pl.ds(0, lanes)],
+            dst_ref=recv_ref.at[c, there, pl.ds(0, lanes)], send_sem=a_out.at[c, off],
+            recv_sem=a_in.at[c, off], device_id=(band, peer), device_id_type=MESH,
+        )
+
+    for c, windows in enumerate(chunks):
+        base = len(windows) * LANES
+        for i, k in enumerate(windows):
+            part = pl.ds(k * width, width)
+            stage[i * LANES:(i + 1) * LANES, :] = dens_ref[:LANES, part]
+            stage[base + i * TAIL:base + i * TAIL + extra, :] = dens_ref[LANES:, part]
+        if len(windows) == 1:
+            stage[base + TAIL:base + 2 * TAIL, :] = jnp.zeros((TAIL, width), f32)
+            stage[base + extra:base + TAIL, :] = jnp.zeros((TAIL - extra, width), f32)
+        hi, lo = two(stage[:base + LANES, :])
+        send[c, :, :base + LANES] = dot_last(perm, hi) + dot_last(perm, lo)
+        cross_copy(c).start()
+    mine = pl.ds(pl.multiple_of(domain * SUBLANES, SUBLANES), SUBLANES)
+    for c, windows in enumerate(chunks):
+        lanes = (len(windows) + 1) * LANES
+        cross_copy(c).wait_recv()
+        send[c, :half, :lanes] += cross[c, :, :lanes]
+        loop(1, lambda off: deal_copy(c, off).start())
+        recv_ref[c, mine, :lanes] = send[c, mine, :lanes]
+        if lanes < recv_ref.shape[2]:
+            recv_ref[c, :, lanes:] = jnp.zeros((half, recv_ref.shape[2] - lanes), f32)
+    for c in range(len(chunks)):
+        loop(1, lambda off: deal_copy(c, off).wait_recv())
+    for c in range(len(chunks)):
+        loop(1, lambda off: deal_copy(c, off).wait_send())
+        cross_copy(c).wait_send()
+    loop(1, lambda off: count_copy(off).wait_send())
+
+def gather_kernel(
+    res_ref, perm_ref, ham_ref, energy_ref, got, cross, x_out, x_in, a_out, a_in, *, domains
+):
+    band, domain = lax.axis_index("band"), lax.axis_index("domain")
+    entries, slots = ham_ref.shape
+    half = SUBLANES * domains
+    width = 2 * half
+    chunks = chunk_plan(slots, width)
+    extra = entries - LANES
+    greet(domains, domain, band)
+
+    def loop(first, function):
+        def step(off, carry):
+            function(off)
+            return carry
+        lax.fori_loop(first, domains, step, 0)
+
+    def back_copy(c, off):
+        lanes = (len(chunks[c]) + 1) * LANES
+        peer = lax.rem(domain + off, domains)
+        rows = pl.ds(pl.multiple_of(peer * SUBLANES, SUBLANES), SUBLANES)
+        there = pl.ds(pl.multiple_of(domain * SUBLANES, SUBLANES), SUBLANES)
+        return pltpu.make_async_remote_copy(
+            src_ref=res_ref.at[c, rows, pl.ds(0, lanes)],
+            dst_ref=got.at[c, there, pl.ds(0, lanes)], send_sem=a_out.at[c, off],
+            recv_sem=a_in.at[c, off], device_id=(band, peer), device_id_type=MESH,
+        )
+
+    def cross_copy(c):
+        lanes = (len(chunks[c]) + 1) * LANES
+        return pltpu.make_async_remote_copy(
+            src_ref=got.at[c, :, pl.ds(0, lanes)],
+            dst_ref=cross.at[c, :, pl.ds(0, lanes)], send_sem=x_out.at[c],
+            recv_sem=x_in.at[c], device_id=(1 - band, domain), device_id_type=MESH,
+        )
+
+    for c in range(len(chunks)):
+        loop(1, lambda off: back_copy(c, off).start())
+    mine = pl.ds(pl.multiple_of(domain * SUBLANES, SUBLANES), SUBLANES)
+    for c in range(len(chunks)):
+        got[c, mine, :] = res_ref[c, mine, :]
+    perm = perm_ref[...]
+
+    def finish(c):
+        cross_copy(c).wait_recv()
+        windows = chunks[c]
+        base = len(windows) * LANES
+
+        def spread(lanes):
+            rows = jnp.concatenate([got[c, :, lanes], cross[c, :, lanes]], axis=0).T
+            hi, lo = two(rows)
+            return jnp.dot(hi, perm, preferred_element_type=f32) + jnp.dot(
+                lo, perm, preferred_element_type=f32
+            )
+
+        tails = spread(slice(base, base + LANES))
+        for i, k in enumerate(windows):
+            part = pl.ds(k * width, width)
+            ham_ref[:LANES, part] = spread(slice(i * LANES, (i + 1) * LANES))
+            ham_ref[LANES:, part] = tails[i * TAIL:i * TAIL + extra]
+            energy_ref[:, part] = tails[i * TAIL + extra:i * TAIL + extra + 1]
+
+    for c in range(len(chunks)):
+        loop(1, lambda off: back_copy(c, off).wait_recv())
+        cross_copy(c).start()
+        if c:
+            finish(c - 1)
+    finish(len(chunks) - 1)
+    for c in range(len(chunks)):
+        loop(1, lambda off: back_copy(c, off).wait_send())
+        cross_copy(c).wait_send()
+
+def atom_kernel(
+    me_ref, recv_ref, all_ref, gy_ref, gyb_ref, pw_ref, pwb_ref, core_ref, weight_ref,
+    res_ref, sel_ref, stack_ref, dens_ref, pts_ref, hi_ref, lo_ref, eacc_ref, back_ref,
+    *, pairs, step, entries, domains, slots
+):
+    atoms = dens_ref.shape[1]
+    rows = pw_ref.shape[1]
+    grid_points = pw_ref.shape[0]
+    couples = gy_ref.shape[0]
+    packed = LANES + TAIL
+    workers = 2 * domains
+    half = SUBLANES * domains
+    width = 2 * half
+    chunks = chunk_plan(slots, width)
+    columns = 2 * atoms // WIDE
+    eacc_ref[...] = jnp.zeros_like(eacc_ref)
+
+    row = lax.broadcasted_iota(jnp.int32, (half, LANES), 0)
+    start = jnp.zeros((half, LANES), jnp.int32)
+    count = jnp.zeros((half, LANES), jnp.int32)
+    for d in range(domains):
+        value = all_ref[d][:1, :]
+        start = start + jnp.where(row >= (d + 1) * SUBLANES, value, 0)
+        count = jnp.where(row // SUBLANES == d, value, count)
+    first = ((me_ref[0] - start) & (workers - 1)) + workers * (row % SUBLANES)
+    lane = lax.broadcasted_iota(jnp.int32, (half, atoms), 1)
+    for c, windows in enumerate(chunks):
+        base = len(windows) * LANES
+        tails = recv_ref[c, :, base:base + LANES].T
+        for i, k in enumerate(windows):
+            slot = first + k * width
+            place = jnp.where(slot < count, (start + slot) // workers, -1)
+            place = jnp.concatenate([place] * (atoms // LANES), axis=1)
+            spot = slice(k * half, (k + 1) * half)
+            sel_ref[spot, :] = jnp.where(place == lane, 1.0, 0.0).astype(bf16)
+            stack_ref[:LANES, spot] = recv_ref[c, :, i * LANES:(i + 1) * LANES].T
+            stack_ref[LANES:, spot] = tails[i * TAIL:(i + 1) * TAIL]
+    hi, lo = two(stack_ref[...])
+    hi = jnp.dot(hi, sel_ref[...], preferred_element_type=f32).astype(bf16)
+    lo = jnp.dot(lo, sel_ref[...], preferred_element_type=f32).astype(bf16)
+    dens_ref[:packed, :] = hi
+    dens_ref[packed:2 * packed, :] = lo
+    dens_ref[2 * packed:, :] = hi
+
+    def mixed(x):
+        ids = lax.broadcasted_iota(jnp.int32, x.shape, 0)
+        hi = x.astype(bf16).astype(f32)
+        low = (ids >= pairs) & (ids < 2 * pairs)
+        return jnp.where(low, x - hi, hi).astype(bf16)
+
+    def body(m, carry):
+        both = jnp.dot(gy_ref[m], dens_ref[...], preferred_element_type=f32)
+        lhs = mixed(jnp.concatenate([both[:rows], both[rows:]], axis=1))
+        back = []
+        for j in range(columns):
+            cols = lhs[:, j * WIDE:(j + 1) * WIDE]
+            pts_ref[j] = jnp.dot(pw_ref[...], cols, preferred_element_type=f32)
+            for g in range(0, grid_points, step):
+                part = pl.ds(g, step)
+                p = pts_ref[j, part, :] + core_ref[part, :]
+                u = p * p + 0.25
+                v = jnp.exp2(jnp.log(u) * (-1.0 / (6.0 * math.log(2.0))))
+                r = v / (7.8 + C_RS * v)
+                v2 = v * v
+                br = 0.44 * r
+                eacc_ref[j, part, :] += (u * v2) * (EX_A + br)
+                pot = (p * v2) * (EX_D + (0.44 + (0.44 * C_RS / 3.0) * r) * r)
+                hi = pot.astype(bf16)
+                hi_ref[j, part, :] = hi
+                lo_ref[j, part, :] = (pot - hi.astype(f32)).astype(bf16)
+            first = jnp.dot(pwb_ref[...], hi_ref[j], preferred_element_type=f32)
+            second = jnp.dot(pwb_ref[:rows, :], lo_ref[j], preferred_element_type=f32)
+            back.append(first[:rows] + first[rows:] + second)
+        back = mixed(jnp.concatenate(back, axis=1))
+        start = pl.multiple_of(m * 2 * rows, 2 * rows)
+        back_ref[pl.ds(start, rows), :] = back[:, :atoms]
+        back_ref[pl.ds(start + rows, rows), :] = back[:, atoms:]
+        return carry
+
+    lax.fori_loop(0, couples, body, 0)
+    ham = jnp.dot(gyb_ref[...], back_ref[...], preferred_element_type=f32)
+    sums = [
+        jnp.sum(eacc_ref[j] * weight_ref[...], axis=0, keepdims=True) for j in range(columns)
+    ]
+    sums = jnp.concatenate(sums, axis=1)
+    energy = -(sums[:, :atoms] + sums[:, atoms:])
+    ids = lax.broadcasted_iota(jnp.int32, (packed, atoms), 0)
+    hi, lo = two(jnp.where(ids == entries, energy, ham))
+    for c, windows in enumerate(chunks):
+        base = len(windows) * LANES
+        tails = []
+        for i, k in enumerate(windows):
+            sel = sel_ref[k * half:(k + 1) * half, :]
+            out = dot_last(sel, hi) + dot_last(sel, lo)
+            res_ref[c, :, i * LANES:(i + 1) * LANES] = out[:, :LANES]
+            tails.append(out[:, LANES:])
+        if len(windows) == 1:
+            tails.append(jnp.zeros((half, TAIL), f32))
+            res_ref[c, :, base + LANES:] = jnp.zeros((half, LANES), f32)
+        res_ref[c, :, base:base + LANES] = jnp.concatenate(tails, axis=1)
+
+def prepare(gaunt, pair_waves, y_table, core, radial_weights):
+    entries = gaunt.shape[0]
+    harmonics, directions = y_table.shape
+    pairs, grid_points = pair_waves.shape
+    rows = round_up(3 * pairs, 16)
+    extra = rows - 3 * pairs
+    packed = LANES + TAIL
+    assert directions % 2 == 0
+    fused = jnp.einsum(
+        "plq,ln->nqp", gaunt.reshape(entries, harmonics, pairs), y_table, precision=highest
+    )
+    fused = jnp.pad(fused, ((0, 0), (0, 0), (0, packed - entries)))
+    hi, lo = split(fused)
+    wide = lambda a, b, c: jnp.pad(
+        jnp.concatenate([a, b, c], axis=1), ((0, 0), (0, extra), (0, 0))
+    )
+    hi3 = wide(hi, hi, hi)
+    lo3 = wide(lo, lo, lo)
+    gy = jnp.concatenate([hi3, hi3, lo3], axis=2).reshape(directions // 2, 2 * rows, 3 * packed)
+    gyb = wide(hi, hi, lo).reshape(directions * rows, packed).T
+    pw_hi, pw_lo = split(pair_waves)
+    pw = jnp.pad(jnp.concatenate([pw_hi, pw_hi, pw_lo], axis=0), ((0, extra), (0, 0))).T
+    point_weight = 4.0 * jnp.pi / directions * radial_weights
+    b_hi, b_lo = split(-point_weight[None, :] * pair_waves)
+    triple = lambda x: jnp.pad(jnp.concatenate([x, x, x], axis=0), ((0, extra), (0, 0)))
+    pwb = jnp.concatenate([triple(b_hi), triple(b_lo)], axis=0)
+    core_wide = jnp.broadcast_to(core[:, None], (grid_points, WIDE))
+    weight_wide = jnp.broadcast_to(point_weight[:, None], (grid_points, WIDE))
+    return gy, gyb, pw, pwb, core_wide, weight_wide
+
+def local(memory):
+    return pl.BlockSpec(memory_space=memory)
+
+def dealt(dens_part, counts, gaunt, pair_waves, y_table, core, radial_weights):
+    domains = lax.axis_size("domain")
+    entries, slots = dens_part.shape[1:]
+    pairs, grid_points = pair_waves.shape
+    half = SUBLANES * domains
+    width = 2 * half
+    chunks = chunk_plan(slots, width)
+    n = len(chunks)
+    lanes = (len(chunks[0]) + 1) * LANES
+    atoms = slots // 3 // 2
+    packed = LANES + TAIL
+    vmem, smem = pltpu.VMEM, pltpu.SMEM
+    dma = pltpu.SemaphoreType.DMA
+    own_count = jnp.broadcast_to(counts.reshape(1, 1), (SUBLANES, LANES))
+    recv, every_count, perm = pl.pallas_call(
+        lambda *refs: scatter_kernel(*refs, domains=domains),
+        out_shape=(
+            jax.ShapeDtypeStruct((n, half, lanes), f32),
+            jax.ShapeDtypeStruct((domains, SUBLANES, LANES), jnp.int32),
+            jax.ShapeDtypeStruct((width, width), bf16),
+        ),
+        in_specs=[local(vmem)] * 2,
+        out_specs=(local(vmem),) * 3,
+        scratch_shapes=[
+            vmem((lanes, width), f32),
+            vmem((n, width, lanes), f32),
+            vmem((n, half, lanes), f32),
+            dma((domains,)), dma((domains,)), dma((n,)), dma((n,)),
+            dma((n, domains)), dma((n, domains)),
+        ],
+        compiler_params=pltpu.CompilerParams(
+            collective_id=0, has_side_effects=True, vmem_limit_bytes=32 * 1024 * 1024
+        ),
+        name="scatter",
+    )(dens_part[0], own_count)
+
+    tables = prepare(gaunt, pair_waves, y_table, core, radial_weights)
+    gyb = tables[1]
+    columns = 2 * atoms // WIDE
+    step = 80 if grid_points % 80 == 0 else grid_points
+    me = (2 * lax.axis_index("domain") + lax.axis_index("band")).reshape(1).astype(jnp.int32)
+    result = pl.pallas_call(
+        lambda *refs: atom_kernel(
+            *refs, pairs=pairs, step=step, entries=entries, domains=domains, slots=slots
+        ),
+        out_shape=jax.ShapeDtypeStruct((n, half, lanes), f32),
+        in_specs=[local(smem)] + [local(vmem)] * 8,
+        out_specs=local(vmem),
+        scratch_shapes=[
+            vmem((slots // 2, atoms), bf16),
+            vmem((packed, slots // 2), f32),
+            vmem((3 * packed, atoms), bf16),
+            vmem((columns, grid_points, WIDE), f32),
+            vmem((columns, grid_points, WIDE), bf16),
+            vmem((columns, grid_points, WIDE), bf16),
+            vmem((columns, grid_points, WIDE), f32),
+            vmem((gyb.shape[1], atoms), bf16),
+        ],
+        compiler_params=pltpu.CompilerParams(vmem_limit_bytes=48 * 1024 * 1024),
+        name="atoms",
+    )(me, recv, every_count, *tables)
+
+    ham, energy = pl.pallas_call(
+        lambda *refs: gather_kernel(*refs, domains=domains),
+        out_shape=(
+            jax.ShapeDtypeStruct((entries, slots), f32),
+            jax.ShapeDtypeStruct((1, slots), f32),
+        ),
+        in_specs=[local(vmem)] * 2,
+        out_specs=(local(vmem),) * 2,
+        scratch_shapes=[
+            vmem((n, half, lanes), f32),
+            vmem((n, half, lanes), f32),
+            dma((n,)), dma((n,)), dma((n, domains)), dma((n, domains)),
+        ],
+        compiler_params=pltpu.CompilerParams(
+            collective_id=1, has_side_effects=True, vmem_limit_bytes=32 * 1024 * 1024
+        ),
+        name="gather",
+    )(result, perm)
+    return ham, energy.reshape(slots)
+
+def fits(bands, domains, entries, slots):
+    workers = bands * domains
+    return (
+        bands == 2
+        and workers & (workers - 1) == 0
+        and (SUBLANES * domains) % LANES == 0
+        and slots % (SUBLANES * workers) == 0
+        and slots % (3 * bands * LANES) == 0
+        and LANES < entries < LANES + TAIL
+    )
+
 def solution(mesh):
+    bands, domains = mesh.shape["band"], mesh.shape["domain"]
+
+    def per_device(dens_part, *rest):
+        entries, slots = dens_part.shape[1:]
+        path = dealt if fits(bands, domains, entries, slots) else general
+        return path(dens_part, *rest)
+
     return jax.shard_map(
         per_device,
         mesh=mesh,

time: 207 us -> 140 us (0.68)
  waiting for transfers between devices: 87.6 us -> 0 us
  Pallas kernels: 43.6 us -> 121 us
  between operations: 17.1 us -> 1.52 us
  local copies, waits for them, and re-layouts: 24.1 us -> 9.24 us
  blocking collectives: 13.8 us -> 0 us
  starting transfers between devices: 10.1 us -> 0 us
  other arithmetic: 9.25 us -> 6.72 us
    pallas_call x1 -> x3, Pallas kernels: 43.6 us -> 121 us  [the longest x1 46.2 us: dealt(): pl.pallas_call(lambda *refs: atom_kernel(*refs, pairs=pairs, step=step, e...]
    all_to_all x2 -> x0, waiting for transfers between devices: 62.7 us -> none  [the longest x1 31.8 us: per_device(): lax.all_to_all(back.reshape(workers, capacity, entries + 1), axes, split_...]
    ppermute x1 -> x0, waiting for transfers between devices: 17.9 us -> none  [per_device(): piece = lax.ppermute(piece, 'band', ring)]
    unnamed x1 -> x0, blocking collectives: 13.8 us -> none
    all_to_all x2 -> x0, starting transfers between devices: 8.52 us -> none  [the longest x1 4.9 us: per_device(): lax.all_to_all(outgoing, axes, split_axis=0, concat_axis=0, tiled=True)]
    reduce_scatter x1 -> x0, waiting for transfers between devices: 6.99 us -> none  [per_device(): lax.psum_scatter(dens_part[0], 'band', scatter_dimension=1, tiled=True)]
    gather x3 -> x0, local copies, waits for them, and re-layouts: 5.08 us -> none  [the longest x1 3.27 us: per_device(): jnp.take(result, jnp.clip(target, 0, atoms - 1).reshape(-1), axis=0, mode...]
    unnamed x21 -> x13, local copies, waits for them, and re-layouts: 7.9 us -> 4.43 us
  transfers between devices with their start and end apart: 4 -> 0, of which waited for: 4 -> 0; matrix products, arithmetic and copies ran while one was open for 7% -> 0% of each run, Pallas kernels for 0% -> 0%
where the time goes in v1:
time: 140 us
  Pallas kernels  121 us (86%)
  local copies, waits for them, and re-layouts  9.24 us (7%)
  other arithmetic  6.72 us (5%)
  between operations  1.52 us (1%)
    pallas_call x1, Pallas kernels, dealt(): pl.pallas_call(lambda *refs: atom_kernel(*refs, pairs=pairs, step=step, e...  46.2 us
    pallas_call x1, Pallas kernels, dealt(): pl.pallas_call(lambda *refs: scatter_kernel(*refs, domains=domains), out_...  40.4 us
    pallas_call x1, Pallas kernels, dealt(): pl.pallas_call(lambda *refs: gather_kernel(*refs, domains=domains), out_s...  34.4 us
    unnamed x13, local copies, waits for them, and re-layouts  4.43 us

profile of v1, /device:TPU:0, one launch (start us, length us, event | category | flops | bytes accessed | tf_op | source)
XLA Modules:
  0.0 139.7 jit_solution(12892740333404922608)
XLA Ops:
  0.6 0.7 broadcast_multiply_fusion
  1.3 0.8 reduce-precision_convert_fusion.1
  2.2 1.2 copy.21
  3.4 0.1 reshape.26
  3.5 1.2 convolution_bitcast_fusion
  4.7 0.2 reduce-precision_convert_fusion
  4.9 1.9 %pad_maximum_fusion = (bf16[50,63,192]{2,0,1:T(8,128)(2,1)}, bf16[50,63,192]{2,0,1:T(8,128)(2,1)S(1)}, bf16[50,63,192]{2,0,1:T(8,128)(2,1)S(1)}) fusion(bf16[50,21,192]{2,0,1:T(8,128)(2,1)S(1)} %get-tuple-element.13, bf16[50,21,192]{2,0,1:T(8,128)(2,1)S(1)} %get-tuple-element.12), kind=kLoop, calls=%fused_computation.3 | loop fusion | flops 3024000 | bytes 4435200 | tf_op jit(solution)/shard_map/concatenate | solution.py:507
  6.8 0.3 pad.25
  7.1 2.3 %fusion.1 = bf16[50,64,576]{2,0,1:T(8,128)(2,1)S(1)} fusion(bf16[50,63,192]{2,0,1:T(8,128)(2,1)S(1)} %get-tuple-element.16, bf16[50,64,192]{2,0,1:T(8,128)(2,1)S(1)} %pad.25), kind=kLoop, calls=%fused_computation.2 | loop fusion | flops 14745600 | bytes 6124800 | tf_op jit(solution)/shard_map/concatenate | solution.py:511
  9.4 2.7 %copy.23 = bf16[50,64,576]{2,1,0:T(8,128)(2,1)} copy(bf16[50,64,576]{2,0,1:T(8,128)(2,1)S(1)} %fusion.1) | data formatting | bytes 7372800 | tf_op jit(solution)/shard_map/concatenate | solution.py:511
  12.1 0.1 copy.26
  12.3 0.1 copy.27
  12.4 0.1 fusion.15.refs_5_
  12.6 0.4 copy.30
  13.0 0.4 pad.27.clone
  13.4 1.0 copy.25
  14.4 1.5 %copy.34 = f32[1,171,2304]{2,1,0:T(8,128)S(1)} copy(f32[1,171,2304]{2,0,1:T(1,128)} %param.7) | data formatting | bytes 3151872
  16.6 40.4 %scatter.1 = (f32[5,128,384]{2,1,0:T(8,128)S(1)}, s32[16,8,128]{2,1,0:T(8,128)S(1)}, bf16[256,256]{1,0:T(8,128)(2,1)S(1)}) custom-call(f32[171,2304]{1,0:T(8,128)S(1)} %bitcast.18, s32[8,128]{1,0:T(8,128)S(1)} %broadcast_in_dim.9.refs_1_), custom_call_target="tpu_custom_call" | custom-call | tf_op jit(solution)/shard_map/scatter/pallas_call | solution.py:540
  57.0 0.1 broadcast_in_dim.11.refs_8_
  57.1 0.1 broadcast_in_dim.10.refs_7_
  57.3 46.2 %atoms.1.refs_0_ = f32[5,128,384]{2,1,0:T(8,128)S(1)} custom-call(s32[1]{0:T(128)} %bitcast.refs_0_, f32[5,128,384]{2,1,0:T(8,128)S(1)} %get-tuple-element.7.refs_1_, s32[16,8,128]{2,1,0:T(8,128)S(1)} %get-tuple-element.8.refs_2_, bf16[25,128,576]{2,1,0:T(8,128)(2,1)} %bitcast.20, bf16[192,3200]{1,0:T(8,128)(2,1)S(1)} %bitcast.19, ...), custom_call_target="tpu_custom_call" | custom-call | tf_op jit(solution)/shard_map/atoms/pallas_call | solution.py:567
  103.5 34.4 %gather.1 = (f32[171,2304]{1,0:T(8,128)S(1)}, f32[1,2304]{1,0:T(1,128)S(1)}) custom-call(f32[5,128,384]{2,1,0:T(8,128)S(1)} %atoms.1.refs_0_, bf16[256,256]{1,0:T(8,128)(2,1)S(1)} %get-tuple-element.9.refs_1_), custom_call_target="tpu_custom_call" | custom-call | tf_op jit(solution)/shard_map/gather/pallas_call | solution.py:588
  137.9 0.6 reduce
  138.5 1.2 copy.37
  (12 shorter events, 0.1 us)
Async XLA Ops:
  0.6 2.9 %copy-start = (f32[25,50]{1,0:T(8,128)S(1)}, f32[25,50]{1,0:T(8,128)}, u32[]{:S(2)}) copy-start(f32[25,50]{1,0:T(8,128)} %param.11) | copy-start | bytes 15004
  9.4 2.8 %copy-start.2 = (f32[21,400]{1,0:T(8,128)S(1)}, f32[21,400]{1,0:T(8,128)}, u32[]{:S(2)}) copy-start(f32[21,400]{1,0:T(8,128)} %param.10) | copy-start | bytes 100804
  9.4 3.1 %copy-start.1 = (bf16[50,63,192]{2,0,1:T(8,128)(2,1)S(1)}, bf16[50,63,192]{2,0,1:T(8,128)(2,1)}, u32[]{:S(2)}) copy-start(bf16[50,63,192]{2,0,1:T(8,128)(2,1)} %get-tuple-element.14) | copy-start | bytes 3628804
  15.9 41.2 %copy-start.3 = (f32[400]{0:T(512)S(1)}, f32[400]{0:T(512)}, u32[]{:S(2)}) copy-start(f32[400]{0:T(512)} %param.12) | copy-start | bytes 4804

commit v2 on v0

--- a/solution.py
+++ b/solution.py
@@ -25,7 +25,7 @@
     hi = lax.reduce_precision(x, 8, 7)
     return hi.astype(bf16), (x - hi).astype(bf16)
 
-def atom_kernel(
+def general_kernel(
     dens_ref, gy_ref, gyb_ref, pw_ref, pwb_ref, core_ref, weight_ref,
     ham_ref, energy_ref, pts_ref, hi_ref, lo_ref, eacc_ref, back_ref, *, pairs, step
 ):
@@ -81,7 +81,7 @@
         -(sums[:, :atoms] + sums[:, atoms:]), energy_ref.shape
     )
 
-def prepare(gaunt, pair_waves, y_table, core, radial_weights):
+def general_tables(gaunt, pair_waves, y_table, core, radial_weights):
     entries = gaunt.shape[0]
     harmonics, directions = y_table.shape
     pairs, grid_points = pair_waves.shape
@@ -110,7 +110,7 @@
     weight_wide = jnp.broadcast_to(point_weight[:, None], (grid_points, WIDE))
     return gy, gyb, pw, pwb, core_wide, weight_wide
 
-def local_energy(columns, tables, pairs):
+def general_energy(columns, tables, pairs):
     entries, atoms = columns.shape
     gy, gyb, pw, pwb, core_wide, weight_wide = tables
     grid_points, rows = pw.shape
@@ -120,7 +120,7 @@
     step = 80 if grid_points % 80 == 0 else grid_points
 
     ham, energy = pl.pallas_call(
-        lambda *refs: atom_kernel(*refs, pairs=pairs, step=step),
+        lambda *refs: general_kernel(*refs, pairs=pairs, step=step),
         out_shape=(
             jax.ShapeDtypeStruct((entries, atoms), f32),
             jax.ShapeDtypeStruct((8, atoms), f32),
@@ -137,7 +137,7 @@
     )(dens, gy, gyb, pw, pwb, core_wide, weight_wide)
     return ham, energy[:1]
 
-def per_device(dens_part, counts, gaunt, pair_waves, y_table, core, radial_weights):
+def general(dens_part, counts, gaunt, pair_waves, y_table, core, radial_weights):
     band_count = lax.axis_size("band")
     domain_count = lax.axis_size("domain")
     workers = band_count * domain_count
@@ -149,7 +149,7 @@
     capacity = -(-share // workers)
     worker_rows = -(-(slot_total // 3) // band_count)
     atoms = round_up(worker_rows, LANES)
-    tables = prepare(gaunt, pair_waves, y_table, core, radial_weights)
+    tables = general_tables(gaunt, pair_waves, y_table, core, radial_weights)
 
     own_cols = lax.psum_scatter(dens_part[0], "band", scatter_dimension=1, tiled=True)
     every_count = lax.all_gather(counts, "domain", axis=0, tiled=True)
@@ -177,7 +177,7 @@
         incoming.reshape(workers * capacity, entries), source * capacity + position, axis=0,
         mode="clip",
     )
-    ham, energy = local_energy(compact.T, tables, pair_waves.shape[0])
+    ham, energy = general_energy(compact.T, tables, pair_waves.shape[0])
     result = jnp.concatenate([ham, energy], axis=0).T
     row = (me - starts) % workers
     first = (starts + row - me) // workers
@@ -200,7 +200,497 @@
     whole = whole.T
     return whole[:entries], whole[entries]
 
+MESH = pl.DeviceIdType.MESH
+SUBLANES = 8
+TAIL = 64
+STEP = 80
+E1 = 0.44 / 7.8
+E2 = 0.44 * C_RS / (3.0 * 7.8 * 7.8)
+
+def chunk_plan(slots, width, odd_first):
+    windows = slots // width
+    lead = windows % 2 if odd_first else 0
+    pieces = [range(lead)] if lead else []
+    return pieces + [range(k, min(k + 2, windows)) for k in range(lead, windows, 2)]
+
+def dot_last(a, b):
+    return lax.dot_general(a, b, (((1,), (1,)), ((), ())), preferred_element_type=f32)
+
+def two(x):
+    hi = x.astype(bf16)
+    return hi, (x - hi.astype(f32)).astype(bf16)
+
+def greet(domains, domain, band):
+    barrier = pltpu.get_barrier_semaphore()
+
+    def hello(off, carry):
+        peer = lax.rem(domain + off, domains)
+        pl.semaphore_signal(barrier, inc=1, device_id=(band, peer), device_id_type=MESH)
+        return carry
+
+    lax.fori_loop(1, domains, hello, 0)
+    pl.semaphore_signal(barrier, inc=1, device_id=(1 - band, domain), device_id_type=MESH)
+    pl.semaphore_wait(barrier, domains)
+
+def whole_kernel(
+    dens_ref, cnt_ref, gaunt_ref, waves_ref, y_ref, core_ref, radial_ref,
+    ham_ref, energy_ref,
+    own_ref, all_ref, perm_ref, stage, send, cross, recv, res_ref, got, cross_back,
+    sel_ref, stack_ref, gpad_ref, ypad_ref, wpad_ref, coef_ref, flow_ref, back_ref,
+    pts_ref, hi_ref, lo_ref, eacc_ref, outs_ref,
+    cnt_out, cnt_in, x_out, x_in, a_out, a_in, rx_out, rx_in, ra_out, ra_in,
+    *, step, domains, depth_of
+):
+    band, domain = lax.axis_index("band"), lax.axis_index("domain")
+    entries, slots = dens_ref.shape[1:]
+    fields = gaunt_ref.shape[1]
+    pairs, grid_points = waves_ref.shape
+    harmonics, directions = y_ref.shape
+    workers = 2 * domains
+    half = SUBLANES * domains
+    width = 2 * half
+    windows_all = slots // width
+    outward = chunk_plan(slots, width, True)
+    homeward = chunk_plan(slots, width, False)
+    extra = entries - LANES
+    atoms = sel_ref.shape[1]
+    tiles = atoms // LANES
+    qp, lp, np_ = round_up(pairs, 8), round_up(harmonics, 16), round_up(directions, 8)
+    nn = round_up(directions, 16)
+    depth = 3 * qp + 8
+    packed = LANES + TAIL
+    couples = directions // 2
+    mine = pl.ds(pl.multiple_of(domain * SUBLANES, SUBLANES), SUBLANES)
+
+    def loop(first, function):
+        def turn(off, carry):
+            function(off)
+            return carry
+        lax.fori_loop(first, domains, turn, 0)
+
+    def lanes_of(windows):
+        return (len(windows) + 1) * LANES
+
+    def count_copy(off):
+        peer = lax.rem(domain + off, domains)
+        return pltpu.make_async_remote_copy(
+            src_ref=own_ref, dst_ref=all_ref.at[domain], send_sem=cnt_out.at[off],
+            recv_sem=cnt_in.at[off], device_id=(band, peer), device_id_type=MESH,
+        )
+
+    def pair_copy(source, target, c, windows, out_sem, in_sem, first):
+        lanes = pl.ds(0, lanes_of(windows))
+        return pltpu.make_async_remote_copy(
+            src_ref=source.at[c, pl.ds(first, half), lanes],
+            dst_ref=target.at[c, :, lanes], send_sem=out_sem.at[c],
+            recv_sem=in_sem.at[c], device_id=(1 - band, domain), device_id_type=MESH,
+        )
+
+    def plane_copy(source, target, c, windows, out_sem, in_sem, off):
+        lanes = pl.ds(0, lanes_of(windows))
+        peer = lax.rem(domain + off, domains)
+        rows = pl.ds(pl.multiple_of(peer * SUBLANES, SUBLANES), SUBLANES)
+        return pltpu.make_async_remote_copy(
+            src_ref=source.at[c, rows, lanes],
+            dst_ref=target.at[c, mine, lanes], send_sem=out_sem.at[c, off],
+            recv_sem=in_sem.at[c, off], device_id=(band, peer), device_id_type=MESH,
+        )
+
+    def sum_copy(c):
+        return pair_copy(send, cross, c, outward[c], x_out, x_in, half)
+
+    def deal_copy(c, off):
+        return plane_copy(send, recv, c, outward[c], a_out, a_in, off)
+
+    def back_copy(c, off):
+        return plane_copy(res_ref, got, c, homeward[c], ra_out, ra_in, off)
+
+    def share_copy(c):
+        return pair_copy(got, cross_back, c, homeward[c], rx_out, rx_in, 0)
+
+    greet(domains, domain, band)
+    own_ref[...] = jnp.full((SUBLANES, LANES), cnt_ref[0], jnp.int32)
+    loop(1, lambda off: count_copy(off).start())
+    all_ref[domain] = own_ref[...]
+    stage[...] = jnp.zeros_like(stage)
+    hi_ref[...] = jnp.zeros_like(hi_ref)
+    lo_ref[...] = jnp.zeros_like(lo_ref)
+    back_ref[...] = jnp.zeros_like(back_ref)
+    flow_ref[...] = jnp.zeros_like(flow_ref)
+    gpad_ref[...] = jnp.zeros_like(gpad_ref)
+    ypad_ref[...] = jnp.zeros_like(ypad_ref)
+    wpad_ref[...] = jnp.zeros_like(wpad_ref)
+    loop(1, lambda off: count_copy(off).wait_recv())
+    start = jnp.zeros((SUBLANES, LANES), jnp.int32)
+    for d in range(domains):
+        start = start + jnp.where(d < domain, all_ref[d], 0)
+    start = start[:1, :1]
+    row = lax.broadcasted_iota(jnp.int32, (width, width), 0)
+    slot = lax.broadcasted_iota(jnp.int32, (width, width), 1)
+    own = row < half
+    row = jnp.where(own, row, row - half)
+    worker = 2 * (row // SUBLANES) + jnp.where(own, band, 1 - band)
+    source = ((worker - start) & (workers - 1)) + workers * (row % SUBLANES)
+    perm = jnp.where(slot == source, 1.0, 0.0).astype(bf16)
+    perm_ref[...] = perm
+    for c, windows in enumerate(outward):
+        base = len(windows) * LANES
+        for i, k in enumerate(windows):
+            part = pl.ds(k * width, width)
+            stage[i * LANES:(i + 1) * LANES, :] = dens_ref[0, :LANES, part]
+            stage[base + i * TAIL:base + i * TAIL + extra, :] = dens_ref[0, LANES:, part]
+            rest = slice(base + i * TAIL + extra, base + (i + 1) * TAIL)
+            stage[rest, :] = jnp.zeros((TAIL - extra, width), f32)
+        if len(windows) == 1:
+            stage[base + TAIL:base + 2 * TAIL, :] = jnp.zeros((TAIL, width), f32)
+        hi, lo = two(stage[:base + LANES, :])
+        send[c, :, :base + LANES] = dot_last(perm, hi) + dot_last(perm, lo)
+        sum_copy(c).start()
+
+    def product(a_hi, a_lo, x):
+        x_hi, x_lo = two(x)
+        return (
+            jnp.dot(a_hi, x_hi, preferred_element_type=f32)
+            + jnp.dot(a_hi, x_lo, preferred_element_type=f32)
+            + jnp.dot(a_lo, x_hi, preferred_element_type=f32)
+        )
+
+    gpad_ref[:entries, :] = gaunt_ref[...]
+    r = lax.broadcasted_iota(jnp.int32, (pairs * lp, fields), 0)
+    col = lax.broadcasted_iota(jnp.int32, (pairs * lp, fields), 1)
+    wanted = jnp.where(r % lp < harmonics, (r % lp) * pairs + r // lp, -1)
+    order = jnp.where(wanted == col, 1.0, 0.0).astype(bf16)
+    g_hi, g_lo = two(gpad_ref[...])
+    into_hi, into_lo = dot_last(order, g_hi).astype(bf16), dot_last(order, g_lo).astype(bf16)
+    out_hi, out_lo = dot_last(g_hi, order).astype(bf16), dot_last(g_lo, order).astype(bf16)
+    ypad_ref[:harmonics, :directions] = y_ref[...]
+    y_hi, y_lo = two(ypad_ref[...])
+    turned = ypad_ref[...].T[:nn, :lp]
+    yt_hi, yt_lo = two(turned)
+
+    point_weight = (4.0 * math.pi / directions) * radial_ref[...]
+    waves = waves_ref[...]
+    waves_hi = waves.astype(bf16).astype(f32)
+    core = core_ref[...]
+    core_hi = core.astype(bf16).astype(f32)
+    core_mid = (core - core_hi).astype(bf16).astype(f32)
+    wpad_ref[:pairs, :grid_points] = waves_hi
+    wpad_ref[qp:qp + pairs, :grid_points] = waves_hi
+    wpad_ref[2 * qp:2 * qp + pairs, :grid_points] = waves - waves_hi
+    wpad_ref[3 * qp:3 * qp + 1, :grid_points] = core_hi
+    wpad_ref[3 * qp + 1:3 * qp + 2, :grid_points] = core_mid
+    wpad_ref[3 * qp + 2:3 * qp + 3, :grid_points] = core - core_hi - core_mid
+    wpad_ref[depth:depth + 1, :grid_points] = point_weight
+    turned = wpad_ref[...].T
+    forward = turned[:grid_points, :depth].astype(bf16)
+    weight = turned[:grid_points, depth:depth + 1]
+    wpad_ref[:qp, :] = jnp.zeros((qp, wpad_ref.shape[1]), f32)
+    wpad_ref[:pairs, :grid_points] = waves * (-E2 * point_weight)
+    b_hi, b_lo = two(wpad_ref[:qp, :grid_points])
+    reverse = jnp.concatenate([b_hi.astype(f32), b_lo.astype(f32)], axis=0).astype(bf16)
+
+    me = 2 * domain + band
+    row = lax.broadcasted_iota(jnp.int32, (half, LANES), 0)
+    held, begun = [], jnp.zeros((1, LANES), jnp.int32)
+    for d in range(domains):
+        value = all_ref[d][:1, :]
+        held.append(jnp.maximum((value - ((me - begun) & (workers - 1)) + workers - 1) // workers, 0))
+        begun = begun + value
+    lane = lax.broadcasted_iota(jnp.int32, (half, atoms), 1)
+    base = jnp.zeros((1, LANES), jnp.int32)
+    for k in range(windows_all):
+        rank = jnp.zeros((half, LANES), jnp.int32) + row % SUBLANES + base
+        live = jnp.zeros((half, LANES), jnp.int32)
+        for d in range(domains):
+            here = jnp.clip(held[d] - SUBLANES * k, 0, SUBLANES)
+            rank = rank + jnp.where(row >= (d + 1) * SUBLANES, here, 0)
+            live = jnp.where(row // SUBLANES == d, here, live)
+            base = base + here
+        rank = jnp.where(row % SUBLANES < live, rank, -1)
+        rank = jnp.concatenate([rank] * tiles, axis=1)
+        sel_ref[k * half:(k + 1) * half, :] = jnp.where(rank == lane, 1.0, 0.0).astype(bf16)
+
+    def deal(c):
+        lanes = lanes_of(outward[c])
+        sum_copy(c).wait_recv()
+        send[c, :half, :lanes] += cross[c, :, :lanes]
+        loop(1, lambda off: deal_copy(c, off).start())
+        recv[c, mine, :lanes] = send[c, mine, :lanes]
+
+    def take(c):
+        loop(1, lambda off: deal_copy(c, off).wait_recv())
+        windows = outward[c]
+        base = len(windows) * LANES
+        tails = recv[c, :, base:base + LANES].T
+        for i, k in enumerate(windows):
+            spot = slice(k * half, (k + 1) * half)
+            stack_ref[:LANES, spot] = recv[c, :, i * LANES:(i + 1) * LANES].T
+            stack_ref[LANES:, spot] = tails[i * TAIL:(i + 1) * TAIL]
+
+    def give(c, known):
+        windows = homeward[c]
+        base = len(windows) * LANES
+        span = slice(0, known * LANES)
+        tails = []
+        for i, k in enumerate(windows):
+            sel = sel_ref[k * half:(k + 1) * half, span]
+            out = dot_last(sel, outs_ref[0, :, span]) + dot_last(sel, outs_ref[1, :, span])
+            res_ref[c, :, i * LANES:(i + 1) * LANES] = out[:, :LANES]
+            tails.append(out[:, LANES:])
+        if len(windows) == 1:
+            tails.append(jnp.zeros((half, TAIL), f32))
+        res_ref[c, :, base:base + LANES] = jnp.concatenate(tails, axis=1)
+        loop(1, lambda off: back_copy(c, off).start())
+        got[c, mine, :base + LANES] = res_ref[c, mine, :base + LANES]
+
+    def share(c):
+        loop(1, lambda off: back_copy(c, off).wait_recv())
+        share_copy(c).start()
+
+    def places(n):
+        return [pl.ds(2 * n + i, qp, stride=np_) for i in range(2)]
+
+    ones = jnp.ones((8, WIDE), f32)
+
+    def enter(n, s):
+        x = jnp.concatenate([flow_ref[at, :] for at in places(n)], axis=1)
+        hi = x.astype(bf16).astype(f32)
+        cols = jnp.concatenate([hi, x - hi, hi, ones], axis=0).astype(bf16)
+        pts_ref[s] = jnp.dot(forward, cols, preferred_element_type=f32)
+
+    def leave(n, s):
+        both = jnp.dot(reverse, hi_ref[s], preferred_element_type=f32)
+        out = both[:qp] + both[qp:] + jnp.dot(b_hi, lo_ref[s], preferred_element_type=f32)
+        for i, at in enumerate(places(n)):
+            back_ref[at, :] = out[:, i * LANES:(i + 1) * LANES]
+
+    def evaluate(s):
+        for g in range(0, grid_points, step):
+            part = pl.ds(g, step)
+            p = pts_ref[s, part, :]
+            u = p * p + 0.25
+            power = jnp.log2(u)
+            t = jnp.exp2(power * (1.0 / 6.0))
+            w = jnp.exp2(power * (-1.0 / 3.0))
+            r = 1.0 / (t + C_RS / 7.8)
+            eacc_ref[s, part, :] += (u * w) * (r + EX_A / E1)
+            pot = (p * w) * ((r + E1 / E2) * r + EX_D / E2)
+            hi = pot.astype(bf16)
+            hi_ref[s, part, :] = hi
+            lo_ref[s, part, :] = (pot - hi.astype(f32)).astype(bf16)
+
+    def compute(i, services):
+        rows = slice(0, -(-(i + 1) * windows_all // tiles) * half)
+        span = slice(i * LANES, (i + 1) * LANES)
+        sel = sel_ref[rows, span]
+        hi, lo = two(stack_ref[:, rows])
+        hi = jnp.dot(hi, sel, preferred_element_type=f32).astype(bf16)
+        lo = jnp.dot(lo, sel, preferred_element_type=f32).astype(bf16)
+        coef_ref[...] = (
+            jnp.dot(into_hi, hi, preferred_element_type=f32)
+            + jnp.dot(into_hi, lo, preferred_element_type=f32)
+            + jnp.dot(into_lo, hi, preferred_element_type=f32)
+        )
+        for q in range(pairs):
+            flow = product(yt_hi, yt_lo, coef_ref[q * lp:(q + 1) * lp, :])
+            flow_ref[q * np_:(q + 1) * np_, :] = flow[:np_]
+        eacc_ref[...] = jnp.zeros_like(eacc_ref)
+        enter(0, 0)
+
+        def body(turn, carry):
+            for at, service in services:
+                @pl.when(turn == at)
+                def _():
+                    service()
+            for s in range(depth_of):
+                n = turn * depth_of + s
+                enter(jnp.minimum(n + 1, couples - 1), (s + 1) % depth_of)
+                leave(jnp.maximum(n - 1, 0), (s - 1) % depth_of)
+                evaluate(s)
+            return carry
+
+        lax.fori_loop(0, couples // depth_of, body, 0)
+        leave(couples - 1, depth_of - 1)
+        for q in range(pairs):
+            coef_ref[q * lp:(q + 1) * lp, :] = product(
+                y_hi[:lp, :np_], y_lo[:lp, :np_], back_ref[q * np_:(q + 1) * np_, :]
+            )
+        ham = product(out_hi, out_lo, coef_ref[...])
+        total = eacc_ref[0]
+        for s in range(1, depth_of):
+            total = total + eacc_ref[s]
+        total = jnp.sum(total * weight, axis=0, keepdims=True)
+        energy = -E1 * (total[:, :LANES] + total[:, LANES:])
+        ids = lax.broadcasted_iota(jnp.int32, (packed, LANES), 0)
+        hi, lo = two(jnp.where(ids == entries, energy, ham))
+        outs_ref[0, :, span] = hi
+        outs_ref[1, :, span] = lo
+
+    def last_needed(i):
+        need = -(-(i + 1) * windows_all // tiles)
+        return next(c for c, windows in enumerate(outward) if windows[-1] + 1 >= need)
+
+    turns = couples // depth_of
+    dealt_to, taken, given, shared = 0, 0, 0, 0
+    for i in range(tiles):
+        last = last_needed(i)
+        while dealt_to <= last:
+            deal(dealt_to)
+            dealt_to += 1
+        if i == 0 and dealt_to < len(outward):
+            deal(dealt_to)
+            dealt_to += 1
+        while taken <= last:
+            take(taken)
+            taken += 1
+        services = []
+        if i == 0:
+            for c in range(dealt_to, len(outward)):
+                spot = min(turns - 1, 1 + 2 * (c - dealt_to))
+                services.append((spot, lambda c=c: deal(c)))
+            dealt_to = len(outward)
+        for c in range(shared, given):
+            services.append((min(turns - 1, 3), lambda c=c: share(c)))
+        shared = given
+        compute(i, services)
+        while given < len(homeward):
+            need = -(-half * (homeward[given][-1] + 1) // LANES)
+            if min(need, tiles) > i + 1:
+                break
+            give(given, min(need, tiles))
+            given += 1
+
+    perm = perm_ref[...]
+
+    def finish(c):
+        share_copy(c).wait_recv()
+        windows = homeward[c]
+        base = len(windows) * LANES
+
+        def spread(lanes):
+            rows = jnp.concatenate([got[c, :, lanes], cross_back[c, :, lanes]], axis=0).T
+            hi, lo = two(rows)
+            return jnp.dot(hi, perm, preferred_element_type=f32) + jnp.dot(
+                lo, perm, preferred_element_type=f32
+            )
+
+        tails = spread(slice(base, base + LANES))
+        for i, k in enumerate(windows):
+            part = pl.ds(k * width, width)
+            ham_ref[:LANES, part] = spread(slice(i * LANES, (i + 1) * LANES))
+            ham_ref[LANES:, part] = tails[i * TAIL:i * TAIL + extra]
+            for j in range(width // LANES):
+                line = k * (width // LANES) + j
+                energy_ref[line:line + 1, :] = tails[
+                    i * TAIL + extra:i * TAIL + extra + 1, j * LANES:(j + 1) * LANES
+                ]
+
+    finished = 0
+    for c in range(shared, len(homeward)):
+        share(c)
+        if c:
+            finish(finished)
+            finished += 1
+    while finished < len(homeward):
+        finish(finished)
+        finished += 1
+    for c in range(len(outward)):
+        loop(1, lambda off: deal_copy(c, off).wait_send())
+        sum_copy(c).wait_send()
+    for c in range(len(homeward)):
+        loop(1, lambda off: back_copy(c, off).wait_send())
+        share_copy(c).wait_send()
+    loop(1, lambda off: count_copy(off).wait_send())
+
+def local(memory):
+    return pl.BlockSpec(memory_space=memory)
+
+def dealt(dens_part, counts, gaunt, pair_waves, y_table, core, radial_weights):
+    domains = lax.axis_size("domain")
+    entries, slots = dens_part.shape[1:]
+    pairs, grid_points = pair_waves.shape
+    harmonics, directions = y_table.shape
+    half = SUBLANES * domains
+    width = 2 * half
+    n = len(chunk_plan(slots, width, True))
+    lanes = 3 * LANES
+    atoms = slots // 3 // 2
+    packed = LANES + TAIL
+    vmem, smem = pltpu.VMEM, pltpu.SMEM
+    dma = pltpu.SemaphoreType.DMA
+    step = next(size for size in (STEP, 16, 8) if grid_points % size == 0)
+    depth_of = next(size for size in (5, 4, 3, 2, 1) if directions // 2 % size == 0)
+    qp, lp = round_up(pairs, 8), round_up(harmonics, 16)
+    np_ = round_up(directions, 8)
+    ham, energy = pl.pallas_call(
+        lambda *refs: whole_kernel(*refs, step=step, domains=domains, depth_of=depth_of),
+        out_shape=(
+            jax.ShapeDtypeStruct((entries, slots), f32),
+            jax.ShapeDtypeStruct((slots // LANES, LANES), f32),
+        ),
+        in_specs=[local(vmem), local(smem)] + [local(vmem)] * 5,
+        out_specs=(local(vmem),) * 2,
+        scratch_shapes=[
+            vmem((SUBLANES, LANES), jnp.int32),
+            vmem((domains, SUBLANES, LANES), jnp.int32),
+            vmem((width, width), bf16),
+            vmem((lanes, width), f32),
+            vmem((n, width, lanes), f32),
+            vmem((n, half, lanes), f32),
+            vmem((n, half, lanes), f32),
+            vmem((n, half, lanes), f32),
+            vmem((n, half, lanes), f32),
+            vmem((n, half, lanes), f32),
+            vmem((slots // 2, atoms), bf16),
+            vmem((packed, slots // 2), f32),
+            vmem((packed, gaunt.shape[1]), f32),
+            vmem((LANES, LANES), f32),
+            vmem((LANES, round_up(grid_points, LANES)), f32),
+            vmem((pairs * lp, LANES), f32),
+            vmem((qp * np_, LANES), f32),
+            vmem((qp * np_, LANES), f32),
+            vmem((depth_of, grid_points, WIDE), f32),
+            vmem((depth_of, grid_points, WIDE), bf16),
+            vmem((depth_of, grid_points, WIDE), bf16),
+            vmem((depth_of, grid_points, WIDE), f32),
+            vmem((2, packed, atoms), bf16),
+            dma((domains,)), dma((domains,)), dma((n,)), dma((n,)),
+            dma((n, domains)), dma((n, domains)), dma((n,)), dma((n,)),
+            dma((n, domains)), dma((n, domains)),
+        ],
+        compiler_params=pltpu.CompilerParams(
+            collective_id=0, has_side_effects=True, vmem_limit_bytes=48 * 1024 * 1024
+        ),
+        name="whole",
+    )(
+        dens_part, counts, gaunt, pair_waves, y_table, core.reshape(1, grid_points),
+        radial_weights.reshape(1, grid_points),
+    )
+    return ham, energy.reshape(slots)
+
+def fits(bands, domains, entries, slots, pairs, grid_points, harmonics, directions):
+    workers = bands * domains
+    return (
+        bands == 2
+        and workers & (workers - 1) == 0
+        and (SUBLANES * domains) % LANES == 0
+        and slots % (SUBLANES * workers) == 0
+        and slots % (3 * bands * LANES) == 0
+        and LANES < entries < LANES + TAIL
+        and directions % 2 == 0
+        and max(harmonics, directions, 3 * pairs + 40) <= LANES
+        and grid_points % SUBLANES == 0
+    )
+
 def solution(mesh):
+    bands, domains = mesh.shape["band"], mesh.shape["domain"]
+
+    def per_device(*arrays):
+        entries, slots = arrays[0].shape[1:]
+        sizes = arrays[3].shape + arrays[4].shape
+        path = dealt if fits(bands, domains, entries, slots, *sizes) else general
+        return path(*arrays)
+
     return jax.shard_map(
         per_device,
         mesh=mesh,

time: 207 us -> 95.5 us (0.46)
  waiting for transfers between devices: 87.6 us -> 0 us
  Pallas kernels: 43.6 us -> 90.1 us
  local copies, waits for them, and re-layouts: 24.1 us -> 3.3 us
  between operations: 17.1 us -> 1.42 us
  blocking collectives: 13.8 us -> 0 us
  starting transfers between devices: 10.1 us -> 0 us
  other arithmetic: 9.25 us -> 0 us
    all_to_all x2 -> x0, waiting for transfers between devices: 62.7 us -> none  [the longest x1 31.8 us: per_device(): lax.all_to_all(back.reshape(workers, capacity, entries + 1), axes, split_...]
    pallas_call x1, Pallas kernels: 43.6 us -> 90.1 us  [dealt(): pl.pallas_call(lambda *refs: whole_kernel(*refs, step=step, domains=domai...]
    ppermute x1 -> x0, waiting for transfers between devices: 17.9 us -> none  [per_device(): piece = lax.ppermute(piece, 'band', ring)]
    unnamed x1 -> x0, blocking collectives: 13.8 us -> none
    all_to_all x2 -> x0, starting transfers between devices: 8.52 us -> none  [the longest x1 4.9 us: per_device(): lax.all_to_all(outgoing, axes, split_axis=0, concat_axis=0, tiled=True)]
    reduce_scatter x1 -> x0, waiting for transfers between devices: 6.99 us -> none  [per_device(): lax.psum_scatter(dens_part[0], 'band', scatter_dimension=1, tiled=True)]
    gather x3 -> x0, local copies, waits for them, and re-layouts: 5.08 us -> none  [the longest x1 3.27 us: per_device(): jnp.take(result, jnp.clip(target, 0, atoms - 1).reshape(-1), axis=0, mode...]
    unnamed x21 -> x13, local copies, waits for them, and re-layouts: 7.9 us -> 3.3 us
  transfers between devices with their start and end apart: 4 -> 0, of which waited for: 4 -> 0; matrix products, arithmetic and copies ran while one was open for 7% -> 0% of each run, Pallas kernels for 0% -> 0%
where the time goes in v2:
time: 95.5 us; the launch traced here: 94.8 us
  Pallas kernels  90.1 us (94%)
  local copies, waits for them, and re-layouts  3.3 us (3%)
  between operations  1.42 us (1%)
    pallas_call x1, Pallas kernels, dealt(): pl.pallas_call(lambda *refs: whole_kernel(*refs, step=step, domains=domai...  90.1 us
    unnamed x13, local copies, waits for them, and re-layouts  3.3 us

profile of v2, /device:TPU:0, one launch (start us, length us, event | category | flops | bytes accessed | tf_op | source)
XLA Modules:
  0.0 94.8 jit_solution(15557401190976728054)
XLA Ops:
  0.6 0.0 copy-start.4
  0.6 0.0 copy-start.3
  0.7 0.0 copy-start.2
  0.7 0.0 copy-start.1
  0.7 0.0 copy-start
  1.4 1.5 %copy.9.refs_0_ = f32[1,171,2304]{2,1,0:T(8,128)S(1)} copy(f32[1,171,2304]{2,0,1:T(1,128)} %param.7) | data formatting | bytes 3151872 | tf_op args[0]
  2.9 0.0 copy-done.4
  2.9 0.0 copy-done.3
  2.9 0.0 copy-done.2
  2.9 0.0 copy-done.1
  2.9 0.0 copy-done
  3.0 90.1 %whole.1 = (f32[171,2304]{1,0:T(8,128)S(1)}, f32[18,128]{1,0:T(8,128)S(1)}) custom-call(f32[1,171,2304]{2,1,0:T(8,128)S(1)} %copy.9.refs_0_, s32[1]{0:T(128)S(6)} %copy.12.refs_1_, f32[171,525]{1,0:T(8,128)S(1)} %copy-done, f32[21,400]{1,0:T(8,128)S(1)} %copy-done.1, f32[25,50]{1,0:T(8,128)S(1)} %copy-done.2, f32[1,400]{1,0:T(1,128)S(1)} %bitcast.4, ...), custom_call_target="tpu_custom_call" | custom-call | tf_op jit(solution)/shard_map/whole/pallas_call | solution.py:625
  93.1 1.2 %copy.13 = f32[171,2304]{1,0:T(8,128)} copy(f32[171,2304]{1,0:T(8,128)S(1)} %get-tuple-element.8) | data formatting | bytes 3151872
  94.2 0.6 copy.14
Async XLA Ops:
  0.6 2.3 %copy-start.4 = (f32[400]{0:T(512)S(1)}, f32[400]{0:T(512)}, u32[]{:S(2)}) copy-start(f32[400]{0:T(512)} %param.13) | copy-start | bytes 4804
  0.6 2.3 %copy-start.3 = (f32[400]{0:T(512)S(1)}, f32[400]{0:T(512)}, u32[]{:S(2)}) copy-start(f32[400]{0:T(512)} %param.12) | copy-start | bytes 4804
  0.7 2.3 %copy-start.2 = (f32[25,50]{1,0:T(8,128)S(1)}, f32[25,50]{1,0:T(8,128)}, u32[]{:S(2)}) copy-start(f32[25,50]{1,0:T(8,128)} %refs_4_.1) | copy-start | bytes 15004
  0.7 2.3 %copy-start.1 = (f32[21,400]{1,0:T(8,128)S(1)}, f32[21,400]{1,0:T(8,128)}, u32[]{:S(2)}) copy-start(f32[21,400]{1,0:T(8,128)} %refs_3_.1) | copy-start | bytes 100804
  0.7 2.3 %copy-start = (f32[171,525]{1,0:T(8,128)S(1)}, f32[171,525]{1,0:T(8,128)}, u32[]{:S(2)}) copy-start(f32[171,525]{1,0:T(8,128)} %refs_2_.1) | copy-start | bytes 1077304

commit v3 on v2

--- a/solution.py
+++ b/solution.py
@@ -204,6 +204,7 @@
 SUBLANES = 8
 TAIL = 64
 STEP = 80
+AHEAD = 2
 E1 = 0.44 / 7.8
 E2 = 0.44 * C_RS / (3.0 * 7.8 * 7.8)
 
@@ -274,8 +275,8 @@
     def count_copy(off):
         peer = lax.rem(domain + off, domains)
         return pltpu.make_async_remote_copy(
-            src_ref=own_ref, dst_ref=all_ref.at[domain], send_sem=cnt_out.at[off],
-            recv_sem=cnt_in.at[off], device_id=(band, peer), device_id_type=MESH,
+            src_ref=own_ref, dst_ref=all_ref.at[domain], send_sem=cnt_out,
+            recv_sem=cnt_in, device_id=(band, peer), device_id_type=MESH,
         )
 
     def pair_copy(source, target, c, windows, out_sem, in_sem, first):
@@ -292,9 +293,31 @@
         rows = pl.ds(pl.multiple_of(peer * SUBLANES, SUBLANES), SUBLANES)
         return pltpu.make_async_remote_copy(
             src_ref=source.at[c, rows, lanes],
-            dst_ref=target.at[c, mine, lanes], send_sem=out_sem.at[c, off],
-            recv_sem=in_sem.at[c, off], device_id=(band, peer), device_id_type=MESH,
+            dst_ref=target.at[c, mine, lanes], send_sem=out_sem.at[c],
+            recv_sem=in_sem.at[c], device_id=(band, peer), device_id_type=MESH,
         )
+
+    def count_all():
+        others = pl.ds(0, domains - 1)
+        return pltpu.make_async_remote_copy(
+            src_ref=all_ref.at[others], dst_ref=all_ref.at[others], send_sem=cnt_out,
+            recv_sem=cnt_in, device_id=(1 - band, domain), device_id_type=MESH,
+        )
+
+    def plane_all(source, target, c, windows, out_sem, in_sem):
+        lanes = pl.ds(0, lanes_of(windows))
+        rows = pl.ds(0, half - SUBLANES)
+        return pltpu.make_async_remote_copy(
+            src_ref=source.at[c, rows, lanes], dst_ref=target.at[c, rows, lanes],
+            send_sem=out_sem.at[c], recv_sem=in_sem.at[c],
+            device_id=(1 - band, domain), device_id_type=MESH,
+        )
+
+    def deal_all(c):
+        return plane_all(send, recv, c, outward[c], a_out, a_in)
+
+    def back_all(c):
+        return plane_all(res_ref, got, c, homeward[c], ra_out, ra_in)
 
     def sum_copy(c):
         return pair_copy(send, cross, c, outward[c], x_out, x_in, half)
@@ -320,7 +343,7 @@
     gpad_ref[...] = jnp.zeros_like(gpad_ref)
     ypad_ref[...] = jnp.zeros_like(ypad_ref)
     wpad_ref[...] = jnp.zeros_like(wpad_ref)
-    loop(1, lambda off: count_copy(off).wait_recv())
+    count_all().wait_recv()
     start = jnp.zeros((SUBLANES, LANES), jnp.int32)
     for d in range(domains):
         start = start + jnp.where(d < domain, all_ref[d], 0)
@@ -347,13 +370,14 @@
         send[c, :, :base + LANES] = dot_last(perm, hi) + dot_last(perm, lo)
         sum_copy(c).start()
 
-    def product(a_hi, a_lo, x):
-        x_hi, x_lo = two(x)
-        return (
-            jnp.dot(a_hi, x_hi, preferred_element_type=f32)
-            + jnp.dot(a_hi, x_lo, preferred_element_type=f32)
-            + jnp.dot(a_lo, x_hi, preferred_element_type=f32)
-        )
+    groups = [range(q, min(q + 2, pairs)) for q in range(0, pairs, 2)]
+
+    def side_by_side(ref, group, size):
+        return jnp.concatenate([ref[q * size:(q + 1) * size, :] for q in group], axis=1)
+
+    def terms(x):
+        hi = x.astype(bf16).astype(f32)
+        return jnp.concatenate([hi, x - hi, hi], axis=0).astype(bf16)
 
     gpad_ref[:entries, :] = gaunt_ref[...]
     r = lax.broadcasted_iota(jnp.int32, (pairs * lp, fields), 0)
@@ -363,10 +387,18 @@
     g_hi, g_lo = two(gpad_ref[...])
     into_hi, into_lo = dot_last(order, g_hi).astype(bf16), dot_last(order, g_lo).astype(bf16)
     out_hi, out_lo = dot_last(g_hi, order).astype(bf16), dot_last(g_lo, order).astype(bf16)
-    ypad_ref[:harmonics, :directions] = y_ref[...]
-    y_hi, y_lo = two(ypad_ref[...])
-    turned = ypad_ref[...].T[:nn, :lp]
-    yt_hi, yt_lo = two(turned)
+    out_all = jnp.concatenate([out_hi, out_lo], axis=0)
+    y = y_ref[...]
+    near = y.astype(bf16).astype(f32)
+    for i, part in enumerate((near, near, y - near)):
+        ypad_ref[i * lp:i * lp + harmonics, :directions] = part
+    turned = ypad_ref[...].T
+    y_in = turned[:nn, :3 * lp].astype(bf16)
+    blocks = [turned[:np_, i * lp:(i + 1) * lp] for i in range(3)]
+    ypad_ref[...] = jnp.zeros_like(ypad_ref)
+    for i, part in enumerate(blocks):
+        ypad_ref[i * np_:(i + 1) * np_, :lp] = part
+    y_out = ypad_ref[...].T[:lp, :3 * np_].astype(bf16)
 
     point_weight = (4.0 * math.pi / directions) * radial_ref[...]
     waves = waves_ref[...]
@@ -418,14 +450,18 @@
         recv[c, mine, :lanes] = send[c, mine, :lanes]
 
     def take(c):
-        loop(1, lambda off: deal_copy(c, off).wait_recv())
+        deal_all(c).wait_recv()
         windows = outward[c]
         base = len(windows) * LANES
-        tails = recv[c, :, base:base + LANES].T
+        tails = two(recv[c, :, base:base + LANES].T)
         for i, k in enumerate(windows):
             spot = slice(k * half, (k + 1) * half)
-            stack_ref[:LANES, spot] = recv[c, :, i * LANES:(i + 1) * LANES].T
-            stack_ref[LANES:, spot] = tails[i * TAIL:(i + 1) * TAIL]
+            mains = two(recv[c, :, i * LANES:(i + 1) * LANES].T)
+            for e in range(2):
+                stack_ref[e * packed:e * packed + LANES, spot] = mains[e]
+                stack_ref[e * packed + LANES:(e + 1) * packed, spot] = tails[e][
+                    i * TAIL:(i + 1) * TAIL
+                ]
 
     def give(c, known):
         windows = homeward[c]
@@ -444,7 +480,7 @@
         got[c, mine, :base + LANES] = res_ref[c, mine, :base + LANES]
 
     def share(c):
-        loop(1, lambda off: back_copy(c, off).wait_recv())
+        back_all(c).wait_recv()
         share_copy(c).start()
 
     def places(n):
@@ -473,7 +509,7 @@
             t = jnp.exp2(power * (1.0 / 6.0))
             w = jnp.exp2(power * (-1.0 / 3.0))
             r = 1.0 / (t + C_RS / 7.8)
-            eacc_ref[s, part, :] += (u * w) * (r + EX_A / E1)
+            eacc_ref[s % eacc_ref.shape[0], part, :] += (u * w) * (r + EX_A / E1)
             pot = (p * w) * ((r + E1 / E2) * r + EX_D / E2)
             hi = pot.astype(bf16)
             hi_ref[s, part, :] = hi
@@ -483,25 +519,27 @@
         rows = slice(0, -(-(i + 1) * windows_all // tiles) * half)
         span = slice(i * LANES, (i + 1) * LANES)
         sel = sel_ref[rows, span]
-        hi, lo = two(stack_ref[:, rows])
-        hi = jnp.dot(hi, sel, preferred_element_type=f32).astype(bf16)
-        lo = jnp.dot(lo, sel, preferred_element_type=f32).astype(bf16)
+        picked = jnp.dot(stack_ref[:, rows], sel, preferred_element_type=f32).astype(bf16)
+        hi, lo = picked[:packed], picked[packed:]
         coef_ref[...] = (
             jnp.dot(into_hi, hi, preferred_element_type=f32)
             + jnp.dot(into_hi, lo, preferred_element_type=f32)
             + jnp.dot(into_lo, hi, preferred_element_type=f32)
         )
-        for q in range(pairs):
-            flow = product(yt_hi, yt_lo, coef_ref[q * lp:(q + 1) * lp, :])
-            flow_ref[q * np_:(q + 1) * np_, :] = flow[:np_]
+        for group in groups:
+            x = side_by_side(coef_ref, group, lp)
+            flow = jnp.dot(y_in, terms(x), preferred_element_type=f32)
+            for i, q in enumerate(group):
+                flow_ref[q * np_:(q + 1) * np_, :] = flow[:np_, i * LANES:(i + 1) * LANES]
         eacc_ref[...] = jnp.zeros_like(eacc_ref)
         enter(0, 0)
 
         def body(turn, carry):
             for at, service in services:
-                @pl.when(turn == at)
-                def _():
-                    service()
+                if at < couples // depth_of:
+                    @pl.when(turn == at)
+                    def _():
+                        service()
             for s in range(depth_of):
                 n = turn * depth_of + s
                 enter(jnp.minimum(n + 1, couples - 1), (s + 1) % depth_of)
@@ -510,14 +548,20 @@
             return carry
 
         lax.fori_loop(0, couples // depth_of, body, 0)
+        for at, service in services:
+            if at >= couples // depth_of:
+                service()
         leave(couples - 1, depth_of - 1)
-        for q in range(pairs):
-            coef_ref[q * lp:(q + 1) * lp, :] = product(
-                y_hi[:lp, :np_], y_lo[:lp, :np_], back_ref[q * np_:(q + 1) * np_, :]
-            )
-        ham = product(out_hi, out_lo, coef_ref[...])
+        for group in groups:
+            x = side_by_side(back_ref, group, np_)
+            coef = jnp.dot(y_out, terms(x), preferred_element_type=f32)
+            for i, q in enumerate(group):
+                coef_ref[q * lp:(q + 1) * lp, :] = coef[:, i * LANES:(i + 1) * LANES]
+        c_hi, c_lo = two(coef_ref[...])
+        ham = jnp.dot(out_all, c_hi, preferred_element_type=f32)
+        ham = ham[:packed] + ham[packed:] + jnp.dot(out_hi, c_lo, preferred_element_type=f32)
         total = eacc_ref[0]
-        for s in range(1, depth_of):
+        for s in range(1, eacc_ref.shape[0]):
             total = total + eacc_ref[s]
         total = jnp.sum(total * weight, axis=0, keepdims=True)
         energy = -E1 * (total[:, :LANES] + total[:, LANES:])
@@ -546,14 +590,14 @@
         services = []
         if i == 0:
             for c in range(dealt_to, len(outward)):
-                spot = min(turns - 1, 1 + 2 * (c - dealt_to))
+                spot = 2 + 3 * (c - dealt_to)
                 services.append((spot, lambda c=c: deal(c)))
             dealt_to = len(outward)
         for c in range(shared, given):
             services.append((min(turns - 1, 3), lambda c=c: share(c)))
         shared = given
         compute(i, services)
-        while given < len(homeward):
+        while i + 1 < tiles and given < len(homeward):
             need = -(-half * (homeward[given][-1] + 1) // LANES)
             if min(need, tiles) > i + 1:
                 break
@@ -585,22 +629,37 @@
                     i * TAIL + extra:i * TAIL + extra + 1, j * LANES:(j + 1) * LANES
                 ]
 
-    finished = 0
+    def sent_out(c):
+        deal_all(c).wait_send()
+        sum_copy(c).wait_send()
+
+    def sent_home(c):
+        back_all(c).wait_send()
+
+    finished, cleared = 0, 0
     for c in range(shared, len(homeward)):
+        while given < min(c + AHEAD, len(homeward)):
+            give(given, tiles)
+            given += 1
+        if c == shared:
+            count_all().wait_send()
+            for e in range(len(outward)):
+                sent_out(e)
         share(c)
         if c:
             finish(finished)
             finished += 1
+        if c > 1:
+            sent_home(cleared)
+            cleared += 1
+    while cleared < len(homeward):
+        sent_home(cleared)
+        cleared += 1
     while finished < len(homeward):
         finish(finished)
         finished += 1
-    for c in range(len(outward)):
-        loop(1, lambda off: deal_copy(c, off).wait_send())
-        sum_copy(c).wait_send()
     for c in range(len(homeward)):
-        loop(1, lambda off: back_copy(c, off).wait_send())
         share_copy(c).wait_send()
-    loop(1, lambda off: count_copy(off).wait_send())
 
 def local(memory):
     return pl.BlockSpec(memory_space=memory)
@@ -642,9 +701,9 @@
             vmem((n, half, lanes), f32),
             vmem((n, half, lanes), f32),
             vmem((slots // 2, atoms), bf16),
-            vmem((packed, slots // 2), f32),
+            vmem((2 * packed, slots // 2), bf16),
             vmem((packed, gaunt.shape[1]), f32),
-            vmem((LANES, LANES), f32),
+            vmem((2 * LANES, LANES), f32),
             vmem((LANES, round_up(grid_points, LANES)), f32),
             vmem((pairs * lp, LANES), f32),
             vmem((qp * np_, LANES), f32),
@@ -652,11 +711,10 @@
             vmem((depth_of, grid_points, WIDE), f32),
             vmem((depth_of, grid_points, WIDE), bf16),
             vmem((depth_of, grid_points, WIDE), bf16),
-            vmem((depth_of, grid_points, WIDE), f32),
+            vmem((2, grid_points, WIDE), f32),
             vmem((2, packed, atoms), bf16),
-            dma((domains,)), dma((domains,)), dma((n,)), dma((n,)),
-            dma((n, domains)), dma((n, domains)), dma((n,)), dma((n,)),
-            dma((n, domains)), dma((n, domains)),
+            dma(()), dma(()), dma((n,)), dma((n,)), dma((n,)), dma((n,)),
+            dma((n,)), dma((n,)), dma((n,)), dma((n,)),
         ],
         compiler_params=pltpu.CompilerParams(
             collective_id=0, has_side_effects=True, vmem_limit_bytes=48 * 1024 * 1024
@@ -678,7 +736,7 @@
         and slots % (3 * bands * LANES) == 0
         and LANES < entries < LANES + TAIL
         and directions % 2 == 0
-        and max(harmonics, directions, 3 * pairs + 40) <= LANES
+        and max(3 * harmonics + 48, 2 * directions, 3 * pairs + 40) <= LANES
         and grid_points % SUBLANES == 0
     )
 

time: 95.5 us -> 90.4 us (0.947)
  Pallas kernels: 90.1 us -> 85.5 us
    pallas_call x1, Pallas kernels: 90.1 us -> 85.5 us  [dealt(): pl.pallas_call(lambda *refs: whole_kernel(*refs, step=step, domains=domai...]
where the time goes in v3:
time: 90.4 us; the launch traced here: 90.2 us
  Pallas kernels  85.5 us (95%)
  local copies, waits for them, and re-layouts  3.3 us (4%)
  between operations  1.42 us (2%)
    pallas_call x1, Pallas kernels, dealt(): pl.pallas_call(lambda *refs: whole_kernel(*refs, step=step, domains=domai...  85.5 us
    unnamed x13, local copies, waits for them, and re-layouts  3.3 us

profile of v3, /device:TPU:0, one launch (start us, length us, event | category | flops | bytes accessed | tf_op | source)
XLA Modules:
  0.0 90.2 jit_solution(17040196841643255544)
XLA Ops:
  0.6 0.0 copy-start.4
  0.6 0.0 copy-start.3
  0.7 0.0 copy-start.2
  0.7 0.0 copy-start.1
  0.7 0.0 copy-start
  1.4 1.5 %copy.9.refs_0_ = f32[1,171,2304]{2,1,0:T(8,128)S(1)} copy(f32[1,171,2304]{2,0,1:T(1,128)} %param.7) | data formatting | bytes 3151872 | tf_op args[0]
  2.9 0.0 copy-done.4
  2.9 0.0 copy-done.3
  2.9 0.0 copy-done.2
  2.9 0.0 copy-done.1
  2.9 0.0 copy-done
  3.0 85.5 %whole.1 = (f32[171,2304]{1,0:T(8,128)S(1)}, f32[18,128]{1,0:T(8,128)S(1)}) custom-call(f32[1,171,2304]{2,1,0:T(8,128)S(1)} %copy.9.refs_0_, s32[1]{0:T(128)S(6)} %copy.12.refs_1_, f32[171,525]{1,0:T(8,128)S(1)} %copy-done, f32[21,400]{1,0:T(8,128)S(1)} %copy-done.1, f32[25,50]{1,0:T(8,128)S(1)} %copy-done.2, f32[1,400]{1,0:T(1,128)S(1)} %bitcast.4, ...), custom_call_target="tpu_custom_call" | custom-call | tf_op jit(solution)/shard_map/whole/pallas_call | solution.py:684
  88.5 1.2 %copy.13 = f32[171,2304]{1,0:T(8,128)} copy(f32[171,2304]{1,0:T(8,128)S(1)} %get-tuple-element.8) | data formatting | bytes 3151872
  89.6 0.6 copy.14
Async XLA Ops:
  0.6 2.3 %copy-start.4 = (f32[400]{0:T(512)S(1)}, f32[400]{0:T(512)}, u32[]{:S(2)}) copy-start(f32[400]{0:T(512)} %param.13) | copy-start | bytes 4804
  0.6 2.3 %copy-start.3 = (f32[400]{0:T(512)S(1)}, f32[400]{0:T(512)}, u32[]{:S(2)}) copy-start(f32[400]{0:T(512)} %param.12) | copy-start | bytes 4804
  0.7 2.3 %copy-start.2 = (f32[25,50]{1,0:T(8,128)S(1)}, f32[25,50]{1,0:T(8,128)}, u32[]{:S(2)}) copy-start(f32[25,50]{1,0:T(8,128)} %refs_4_.1) | copy-start | bytes 15004
  0.7 2.3 %copy-start.1 = (f32[21,400]{1,0:T(8,128)S(1)}, f32[21,400]{1,0:T(8,128)}, u32[]{:S(2)}) copy-start(f32[21,400]{1,0:T(8,128)} %refs_3_.1) | copy-start | bytes 100804
  0.7 2.3 %copy-start = (f32[171,525]{1,0:T(8,128)S(1)}, f32[171,525]{1,0:T(8,128)}, u32[]{:S(2)}) copy-start(f32[171,525]{1,0:T(8,128)} %refs_2_.1) | copy-start | bytes 1077304

commit v4 on v3

--- a/solution.py
+++ b/solution.py
@@ -204,6 +204,8 @@
 SUBLANES = 8
 TAIL = 64
 STEP = 80
+EAGER = True
+SPOT = 2
 AHEAD = 2
 E1 = 0.44 / 7.8
 E2 = 0.44 * C_RS / (3.0 * 7.8 * 7.8)
@@ -237,7 +239,7 @@
     dens_ref, cnt_ref, gaunt_ref, waves_ref, y_ref, core_ref, radial_ref,
     ham_ref, energy_ref,
     own_ref, all_ref, perm_ref, stage, send, cross, recv, res_ref, got, cross_back,
-    sel_ref, stack_ref, gpad_ref, ypad_ref, wpad_ref, coef_ref, flow_ref, back_ref,
+    sel_ref, stack_ref, gpad_ref, ypad_ref, wpad_ref, coef_ref, end_ref, flow_ref, back_ref,
     pts_ref, hi_ref, lo_ref, eacc_ref, outs_ref,
     cnt_out, cnt_in, x_out, x_in, a_out, a_in, rx_out, rx_in, ra_out, ra_in,
     *, step, domains, depth_of
@@ -264,10 +266,8 @@
     mine = pl.ds(pl.multiple_of(domain * SUBLANES, SUBLANES), SUBLANES)
 
     def loop(first, function):
-        def turn(off, carry):
+        for off in range(first, domains):
             function(off)
-            return carry
-        lax.fori_loop(first, domains, turn, 0)
 
     def lanes_of(windows):
         return (len(windows) + 1) * LANES
@@ -332,7 +332,7 @@
         return pair_copy(got, cross_back, c, homeward[c], rx_out, rx_in, 0)
 
     greet(domains, domain, band)
-    own_ref[...] = jnp.full((SUBLANES, LANES), cnt_ref[0], jnp.int32)
+    own_ref[...] = jnp.full((1, LANES), cnt_ref[0], jnp.int32)
     loop(1, lambda off: count_copy(off).start())
     all_ref[domain] = own_ref[...]
     stage[...] = jnp.zeros_like(stage)
@@ -344,7 +344,7 @@
     ypad_ref[...] = jnp.zeros_like(ypad_ref)
     wpad_ref[...] = jnp.zeros_like(wpad_ref)
     count_all().wait_recv()
-    start = jnp.zeros((SUBLANES, LANES), jnp.int32)
+    start = jnp.zeros((1, LANES), jnp.int32)
     for d in range(domains):
         start = start + jnp.where(d < domain, all_ref[d], 0)
     start = start[:1, :1]
@@ -492,11 +492,11 @@
         x = jnp.concatenate([flow_ref[at, :] for at in places(n)], axis=1)
         hi = x.astype(bf16).astype(f32)
         cols = jnp.concatenate([hi, x - hi, hi, ones], axis=0).astype(bf16)
-        pts_ref[s] = jnp.dot(forward, cols, preferred_element_type=f32)
+        pts_ref[s, :grid_points, :] = jnp.dot(forward, cols, preferred_element_type=f32)
 
     def leave(n, s):
-        both = jnp.dot(reverse, hi_ref[s], preferred_element_type=f32)
-        out = both[:qp] + both[qp:] + jnp.dot(b_hi, lo_ref[s], preferred_element_type=f32)
+        both = jnp.dot(reverse, hi_ref[s, :grid_points, :], preferred_element_type=f32)
+        out = both[:qp] + both[qp:] + jnp.dot(b_hi, lo_ref[s, :grid_points, :], preferred_element_type=f32)
         for i, at in enumerate(places(n)):
             back_ref[at, :] = out[:, i * LANES:(i + 1) * LANES]
 
@@ -515,7 +515,7 @@
             hi_ref[s, part, :] = hi
             lo_ref[s, part, :] = (pot - hi.astype(f32)).astype(bf16)
 
-    def compute(i, services):
+    def prologue(i):
         rows = slice(0, -(-(i + 1) * windows_all // tiles) * half)
         span = slice(i * LANES, (i + 1) * LANES)
         sel = sel_ref[rows, span]
@@ -529,11 +529,12 @@
         for group in groups:
             x = side_by_side(coef_ref, group, lp)
             flow = jnp.dot(y_in, terms(x), preferred_element_type=f32)
-            for i, q in enumerate(group):
-                flow_ref[q * np_:(q + 1) * np_, :] = flow[:np_, i * LANES:(i + 1) * LANES]
+            for e, q in enumerate(group):
+                flow_ref[q * np_:(q + 1) * np_, :] = flow[:np_, e * LANES:(e + 1) * LANES]
         eacc_ref[...] = jnp.zeros_like(eacc_ref)
         enter(0, 0)
 
+    def main(services):
         def body(turn, carry):
             for at, service in services:
                 if at < couples // depth_of:
@@ -552,17 +553,20 @@
             if at >= couples // depth_of:
                 service()
         leave(couples - 1, depth_of - 1)
+
+    def epilogue(i):
+        span = slice(i * LANES, (i + 1) * LANES)
         for group in groups:
             x = side_by_side(back_ref, group, np_)
             coef = jnp.dot(y_out, terms(x), preferred_element_type=f32)
-            for i, q in enumerate(group):
-                coef_ref[q * lp:(q + 1) * lp, :] = coef[:, i * LANES:(i + 1) * LANES]
-        c_hi, c_lo = two(coef_ref[...])
+            for e, q in enumerate(group):
+                end_ref[q * lp:(q + 1) * lp, :] = coef[:, e * LANES:(e + 1) * LANES]
+        c_hi, c_lo = two(end_ref[...])
         ham = jnp.dot(out_all, c_hi, preferred_element_type=f32)
         ham = ham[:packed] + ham[packed:] + jnp.dot(out_hi, c_lo, preferred_element_type=f32)
-        total = eacc_ref[0]
+        total = eacc_ref[0, :grid_points, :]
         for s in range(1, eacc_ref.shape[0]):
-            total = total + eacc_ref[s]
+            total = total + eacc_ref[s, :grid_points, :]
         total = jnp.sum(total * weight, axis=0, keepdims=True)
         energy = -E1 * (total[:, :LANES] + total[:, LANES:])
         ids = lax.broadcasted_iota(jnp.int32, (packed, LANES), 0)
@@ -581,28 +585,31 @@
         while dealt_to <= last:
             deal(dealt_to)
             dealt_to += 1
-        if i == 0 and dealt_to < len(outward):
+        if i == 0 and dealt_to < len(outward) and EAGER:
             deal(dealt_to)
             dealt_to += 1
         while taken <= last:
             take(taken)
             taken += 1
+        if i:
+            epilogue(i - 1)
+        prologue(i)
+        while i and given < len(homeward):
+            need = -(-half * (homeward[given][-1] + 1) // LANES)
+            if min(need, tiles) > i:
+                break
+            give(given, min(need, tiles))
+            given += 1
         services = []
         if i == 0:
             for c in range(dealt_to, len(outward)):
-                spot = 2 + 3 * (c - dealt_to)
-                services.append((spot, lambda c=c: deal(c)))
+                services.append((SPOT + 3 * (c - dealt_to), lambda c=c: deal(c)))
             dealt_to = len(outward)
         for c in range(shared, given):
             services.append((min(turns - 1, 3), lambda c=c: share(c)))
         shared = given
-        compute(i, services)
-        while i + 1 < tiles and given < len(homeward):
-            need = -(-half * (homeward[given][-1] + 1) // LANES)
-            if min(need, tiles) > i + 1:
-                break
-            give(given, min(need, tiles))
-            given += 1
+        main(services)
+    epilogue(tiles - 1)
 
     perm = perm_ref[...]
 
@@ -690,8 +697,8 @@
         in_specs=[local(vmem), local(smem)] + [local(vmem)] * 5,
         out_specs=(local(vmem),) * 2,
         scratch_shapes=[
-            vmem((SUBLANES, LANES), jnp.int32),
-            vmem((domains, SUBLANES, LANES), jnp.int32),
+            vmem((1, LANES), jnp.int32),
+            vmem((domains, 1, LANES), jnp.int32),
             vmem((width, width), bf16),
             vmem((lanes, width), f32),
             vmem((n, width, lanes), f32),
@@ -706,12 +713,13 @@
             vmem((2 * LANES, LANES), f32),
             vmem((LANES, round_up(grid_points, LANES)), f32),
             vmem((pairs * lp, LANES), f32),
+            vmem((pairs * lp, LANES), f32),
             vmem((qp * np_, LANES), f32),
             vmem((qp * np_, LANES), f32),
-            vmem((depth_of, grid_points, WIDE), f32),
-            vmem((depth_of, grid_points, WIDE), bf16),
-            vmem((depth_of, grid_points, WIDE), bf16),
-            vmem((2, grid_points, WIDE), f32),
+            vmem((depth_of, grid_points + 8, WIDE), f32),
+            vmem((depth_of, grid_points + 16, WIDE), bf16),
+            vmem((depth_of, grid_points + 16, WIDE), bf16),
+            vmem((2, grid_points + 8, WIDE), f32),
             vmem((2, packed, atoms), bf16),
             dma(()), dma(()), dma((n,)), dma((n,)), dma((n,)), dma((n,)),
             dma((n,)), dma((n,)), dma((n,)), dma((n,)),

time: 90.4 us -> 89.4 us (0.989)
  Pallas kernels: 85.5 us -> 84.5 us
    pallas_call x1, Pallas kernels: 85.5 us -> 84.5 us  [dealt(): pl.pallas_call(lambda *refs: whole_kernel(*refs, step=step, domains=domai...]
where the time goes in v4:
time: 89.4 us; the launch traced here: 89.2 us
  Pallas kernels  84.5 us (95%)
  local copies, waits for them, and re-layouts  3.3 us (4%)
  between operations  1.42 us (2%)
    pallas_call x1, Pallas kernels, dealt(): pl.pallas_call(lambda *refs: whole_kernel(*refs, step=step, domains=domai...  84.5 us
    unnamed x13, local copies, waits for them, and re-layouts  3.3 us

profile of v4, /device:TPU:0, one launch (start us, length us, event | category | flops | bytes accessed | tf_op | source)
XLA Modules:
  0.0 89.2 jit_solution(7771908483065893207)
XLA Ops:
  0.6 0.0 copy-start.4
  0.6 0.0 copy-start.3
  0.7 0.0 copy-start.2
  0.7 0.0 copy-start.1
  0.7 0.0 copy-start
  1.4 1.5 %copy.9.refs_0_ = f32[1,171,2304]{2,1,0:T(8,128)S(1)} copy(f32[1,171,2304]{2,0,1:T(1,128)} %param.7) | data formatting | bytes 3151872 | tf_op args[0]
  2.9 0.0 copy-done.4
  2.9 0.0 copy-done.3
  2.9 0.0 copy-done.2
  2.9 0.0 copy-done.1
  2.9 0.0 copy-done
  3.0 84.5 %whole.1 = (f32[171,2304]{1,0:T(8,128)S(1)}, f32[18,128]{1,0:T(8,128)S(1)}) custom-call(f32[1,171,2304]{2,1,0:T(8,128)S(1)} %copy.9.refs_0_, s32[1]{0:T(128)S(6)} %copy.12.refs_1_, f32[171,525]{1,0:T(8,128)S(1)} %copy-done, f32[21,400]{1,0:T(8,128)S(1)} %copy-done.1, f32[25,50]{1,0:T(8,128)S(1)} %copy-done.2, f32[1,400]{1,0:T(1,128)S(1)} %bitcast.4, ...), custom_call_target="tpu_custom_call" | custom-call | tf_op jit(solution)/shard_map/whole/pallas_call | solution.py:691
  87.4 1.2 %copy.13 = f32[171,2304]{1,0:T(8,128)} copy(f32[171,2304]{1,0:T(8,128)S(1)} %get-tuple-element.8) | data formatting | bytes 3151872
  88.6 0.6 copy.14
Async XLA Ops:
  0.6 2.3 %copy-start.4 = (f32[400]{0:T(512)S(1)}, f32[400]{0:T(512)}, u32[]{:S(2)}) copy-start(f32[400]{0:T(512)} %param.13) | copy-start | bytes 4804
  0.6 2.3 %copy-start.3 = (f32[400]{0:T(512)S(1)}, f32[400]{0:T(512)}, u32[]{:S(2)}) copy-start(f32[400]{0:T(512)} %param.12) | copy-start | bytes 4804
  0.7 2.3 %copy-start.2 = (f32[25,50]{1,0:T(8,128)S(1)}, f32[25,50]{1,0:T(8,128)}, u32[]{:S(2)}) copy-start(f32[25,50]{1,0:T(8,128)} %refs_4_.1) | copy-start | bytes 15004
  0.7 2.3 %copy-start.1 = (f32[21,400]{1,0:T(8,128)S(1)}, f32[21,400]{1,0:T(8,128)}, u32[]{:S(2)}) copy-start(f32[21,400]{1,0:T(8,128)} %refs_3_.1) | copy-start | bytes 100804
  0.7 2.3 %copy-start = (f32[171,525]{1,0:T(8,128)S(1)}, f32[171,525]{1,0:T(8,128)}, u32[]{:S(2)}) copy-start(f32[171,525]{1,0:T(8,128)} %refs_2_.1) | copy-start | bytes 1077304
